TPU v7x, 32 devices: a 4x4x1 block of a 4x4x8 slice. The times are simulated.
32 devices in a mesh: dp: 1 (over z), tp: 4 (over y), cp: 8 (over x, core).
Axes of the slice: x: 4, y: 4, z: 1, core: 2. Of those that a mesh axis runs over, the one named last changes fastest.
The devices are a block of a 4x4x8 slice.
Arguments:
- hidden_in: bfloat16 [512, 3072], P(('dp', 'cp', 'tp'))
- positions: int32 [512], P(('dp', 'cp', 'tp'))
- cache_len: int32 [1], P('dp')
- cache_k: bfloat16 [32768, 1024], P(('dp', 'cp', 'tp'))
- cache_v: bfloat16 [32768, 1024], P(('dp', 'cp', 'tp'))
- norm1_gain: bfloat16 [3072], replicated
- w_query: bfloat16 [3072, 3072], P(None, 'tp')
- w_key: bfloat16 [3072, 1024], P(None, 'tp')
- w_value: bfloat16 [3072, 1024], P(None, 'tp')
- w_out: bfloat16 [3072, 3072], P('tp')
- norm2_gain: bfloat16 [3072], replicated
- w_gate: bfloat16 [3072, 8192], P(None, 'tp')
- w_up: bfloat16 [3072, 8192], P(None, 'tp')
- w_down: bfloat16 [8192, 3072], P('tp')
Outputs:
- output: bfloat16 [512, 3072], P(('dp', 'cp', 'tp'))
All inputs are finite; a program needn't handle non-finite values.
Results may differ from a plain program's by a relative error of at most 0.0110867.
Values are sent between devices in bfloat16 or wider.
A program may use at most 768 MiB of HBM per device.

v0:
```python
import math
import jax
import jax.numpy as jnp
from jax import lax
from jax.sharding import PartitionSpec as P

HEAD_DIM = 128
ROPE_BASE = 500000.0
NORM_EPS = 1e-5


def rms_norm(hidden, norm_gain):
    values = hidden.astype(jnp.float32)
    inv_rms = lax.rsqrt(jnp.mean(values * values, axis=-1, keepdims=True) + NORM_EPS)
    return (values * inv_rms * norm_gain.astype(jnp.float32)).astype(jnp.bfloat16)


def rotary(projected, positions):
    half_dim = HEAD_DIM // 2
    inv_freq = 1.0 / (ROPE_BASE ** (jnp.arange(half_dim, dtype=jnp.float32) * (2.0 / HEAD_DIM)))
    angles = positions.astype(jnp.float32)[:, None] * inv_freq[None, :]
    expand = (angles.shape[0],) + (1,) * (projected.ndim - 2) + (half_dim,)
    cos_table = jnp.cos(angles).reshape(expand)
    sin_table = jnp.sin(angles).reshape(expand)
    first_half = projected[..., :half_dim]
    second_half = projected[..., half_dim:]
    rotated = jnp.concatenate([first_half * cos_table - second_half * sin_table, second_half * cos_table + first_half * sin_table], axis=-1)
    return rotated.astype(jnp.bfloat16)


def attend_rows(block_queries, block_pos, cache_keys, cache_values, cache_valid, new_keys, new_values, all_pos):
    score_scale = 1.0 / math.sqrt(HEAD_DIM)
    cache_scores = jnp.einsum('rkgd,skd->krgs', block_queries, cache_keys, preferred_element_type=jnp.float32) * score_scale
    new_scores = jnp.einsum('rkgd,skd->krgs', block_queries, new_keys, preferred_element_type=jnp.float32) * score_scale
    cache_scores = jnp.where(cache_valid, cache_scores, -jnp.inf)
    causal = all_pos[None, None, None, :] <= block_pos[None, :, None, None]
    new_scores = jnp.where(causal, new_scores, -jnp.inf)
    row_max = jnp.maximum(jnp.max(cache_scores, axis=-1, keepdims=True), jnp.max(new_scores, axis=-1, keepdims=True))
    cache_probs = jnp.exp(cache_scores - row_max)
    new_probs = jnp.exp(new_scores - row_max)
    normalizer = jnp.sum(cache_probs, axis=-1, keepdims=True) + jnp.sum(new_probs, axis=-1, keepdims=True)
    weighted = jnp.einsum('krgs,skd->krgd', cache_probs.astype(jnp.bfloat16), cache_values, preferred_element_type=jnp.float32)
    weighted = weighted + jnp.einsum('krgs,skd->krgd', new_probs.astype(jnp.bfloat16), new_values, preferred_element_type=jnp.float32)
    return jnp.transpose((weighted / normalizer).astype(jnp.bfloat16), (1, 0, 2, 3))


def solution(mesh):
    tp_size = mesh.shape['tp']
    token_spec = P(('dp', 'cp', 'tp'), None)
    column_spec = P(None, 'tp')
    row_spec = P('tp', None)

    def device_layer(hidden_loc, pos_loc, cache_len, cache_k, cache_v, norm1_gain, w_query, w_key, w_value, w_out, norm2_gain, w_gate, w_up, w_down):
        shard_rows = hidden_loc.shape[0]
        kv_local = w_key.shape[1] // HEAD_DIM
        groups = w_query.shape[1] // w_key.shape[1]
        normed = rms_norm(hidden_loc, norm1_gain)
        group_in = lax.all_gather(normed, 'tp', axis=0, tiled=True)
        group_pos = lax.all_gather(pos_loc, 'tp', axis=0, tiled=True)
        group_rows = group_in.shape[0]
        queries = rotary(jnp.dot(group_in, w_query, preferred_element_type=jnp.float32).reshape(group_rows, kv_local, groups, HEAD_DIM), group_pos)
        keys_loc = rotary(jnp.dot(group_in, w_key, preferred_element_type=jnp.float32).reshape(group_rows, kv_local, HEAD_DIM), group_pos)
        values_loc = jnp.dot(group_in, w_value, preferred_element_type=jnp.float32).astype(jnp.bfloat16).reshape(group_rows, kv_local, HEAD_DIM)
        new_keys = lax.all_gather(keys_loc, 'cp', axis=0, tiled=True)
        new_values = lax.all_gather(values_loc, 'cp', axis=0, tiled=True)
        all_pos = lax.all_gather(group_pos, 'cp', axis=0, tiled=True)
        cache_keys = lax.all_gather(lax.all_to_all(cache_k, 'tp', 1, 0, tiled=True), 'cp', axis=0, tiled=True).reshape(-1, kv_local, HEAD_DIM)
        cache_values = lax.all_gather(lax.all_to_all(cache_v, 'tp', 1, 0, tiled=True), 'cp', axis=0, tiled=True).reshape(-1, kv_local, HEAD_DIM)
        cache_valid = jnp.arange(cache_keys.shape[0]) < cache_len[0]
        block_queries = queries.reshape(tp_size, shard_rows, kv_local, groups, HEAD_DIM)
        block_pos = group_pos.reshape(tp_size, shard_rows)

        def attend_block(block_item):
            return attend_rows(block_item[0], block_item[1], cache_keys, cache_values, cache_valid, new_keys, new_values, all_pos)

        attended = lax.map(attend_block, (block_queries, block_pos)).reshape(group_rows, kv_local * groups * HEAD_DIM)
        attn_part = jnp.dot(attended, w_out, preferred_element_type=jnp.float32)
        residual_mid = (hidden_loc.astype(jnp.float32) + lax.psum_scatter(attn_part, 'tp', scatter_dimension=0, tiled=True)).astype(jnp.bfloat16)
        group_mid = lax.all_gather(rms_norm(residual_mid, norm2_gain), 'tp', axis=0, tiled=True)
        gate_proj = jnp.dot(group_mid, w_gate, preferred_element_type=jnp.float32)
        up_proj = jnp.dot(group_mid, w_up, preferred_element_type=jnp.float32)
        hidden_mlp = (jax.nn.silu(gate_proj) * up_proj).astype(jnp.bfloat16)
        mlp_part = jnp.dot(hidden_mlp, w_down, preferred_element_type=jnp.float32)
        return (residual_mid.astype(jnp.float32) + lax.psum_scatter(mlp_part, 'tp', scatter_dimension=0, tiled=True)).astype(jnp.bfloat16)

    return jax.shard_map(device_layer, mesh=mesh, in_specs=(token_spec, P(('dp', 'cp', 'tp')), P('dp'), token_spec, token_spec, P(), column_spec, column_spec, column_spec, row_spec, P(), column_spec, column_spec, row_spec), out_specs=token_spec, check_vma=False)
```

profile of v0, /device:TPU:98, one launch (start us, length us, event | category | flops | bytes accessed | tf_op | source)
XLA Modules:
  0.0 477.7 jit_solution(5586534207881813165)
XLA Ops:
  10.6 32.4 %all_to_all.38 = bf16[1024,4,256]{0,2,1:T(8,128)(2,1)} all-to-all(bf16[1024,4,256]{0,2,1:T(8,128)(2,1)} %bitcast.110), channel_id=1, replica_groups=mesh['dp'=1,'tp'=4,'cp'=8] {'tp'}, dimensions={1} | all-to-all | bytes 4194304 | tf_op jit(solution)/shard_map/all_to_all | solution.py:67
  47.1 4.1 copy.36
  51.2 29.9 %all_to_all.39 = bf16[1024,4,256]{0,2,1:T(8,128)(2,1)} all-to-all(bf16[1024,4,256]{0,2,1:T(8,128)(2,1)} %bitcast.111), channel_id=1, replica_groups=mesh['dp'=1,'tp'=4,'cp'=8] {'tp'}, dimensions={1} | all-to-all | bytes 4194304 | tf_op jit(solution)/shard_map/all_to_all | solution.py:68
  86.7 6.7 %all-reduce = s32[64]{0:T(128)S(1)} all-reduce(s32[64]{0:T(128)S(1)} %dynamic-update-slice), channel_id=1, replica_groups=mesh['dp'=1,'tp'=4,'cp'=8] {'tp'}, use_global_device_ids=true, to_apply=%add | all-reduce | flops 64 | bytes 512
  93.7 12.8 %all_gather.24 = bf16[64,3072]{1,0:T(8,128)(2,1)S(1)} all-gather(bf16[16,3072]{1,0:T(8,128)(2,1)S(1)} %fusion.40), channel_id=1, replica_groups=mesh['dp'=1,'tp'=4,'cp'=8] {'tp'}, dimensions={0}, use_global_device_ids=true | all-gather | bytes 491520 | tf_op jit(solution)/shard_map/all_gather | solution.py:58
  114.1 8.3 %all-reduce.1 = s32[512]{0:T(512)S(1)} all-reduce(s32[512]{0:T(512)S(1)} %dynamic-update-slice.1), channel_id=1, replica_groups=mesh['dp'=1,'tp'=4,'cp'=8] {'cp'}, use_global_device_ids=true, to_apply=%add.1 | all-reduce | flops 512 | bytes 4096
  122.6 22.8 %all_gather.28 = bf16[512,2,128]{2,0,1:T(8,128)(2,1)S(1)} all-gather(bf16[64,2,128]{2,0,1:T(8,128)(2,1)S(1)} %pad_maximum_fusion.1), channel_id=1, replica_groups=mesh['dp'=1,'tp'=4,'cp'=8] {'cp'}, dimensions={0}, use_global_device_ids=true | all-gather | bytes 294912 | tf_op jit(solution)/shard_map/all_gather | solution.py:64
  145.4 22.2 %all_gather.30 = bf16[512,2,128]{2,0,1:T(8,128)(2,1)S(1)} all-gather(bf16[64,2,128]{2,0,1:T(8,128)(2,1)S(1)} %bitcast.114), channel_id=1, replica_groups=mesh['dp'=1,'tp'=4,'cp'=8] {'cp'}, dimensions={0}, use_global_device_ids=true | all-gather | bytes 294912 | tf_op jit(solution)/shard_map/all_gather | solution.py:65
  167.8 21.2 %copy.33 = bf16[32768,256]{0,1:T(8,128)(2,1)} copy(bf16[32768,256]{1,0:T(8,128)(2,1)} %all-gather.3.cloned.1.call-done) | data formatting | bytes 33554432 | tf_op jit(solution)/shard_map/all_gather | solution.py:67
  189.0 21.2 %copy.41 = bf16[32768,2,128]{2,0,1:T(8,128)(2,1)} copy(bf16[32768,2,128]{0,2,1:T(8,128)(2,1)} %bitcast.104) | data formatting | bytes 33554432
  210.2 5.5 %all-gather.5.cloned.1.call-done = bf16[32768,256]{1,0:T(8,128)(2,1)} async-done(((bf16[4096,256]{1,0:T(8,128)(2,1)}), bf16[32768,256]{1,0:T(8,128)(2,1)}) %all-gather.5.cloned.1.call-update) | async-done | bytes 16777232 | tf_op jit(solution)/shard_map/all_gather | solution.py:68
  215.7 21.2 %copy.38 = bf16[32768,256]{0,1:T(8,128)(2,1)} copy(bf16[32768,256]{1,0:T(8,128)(2,1)} %all-gather.5.cloned.1.call-done) | data formatting | bytes 33554432 | tf_op jit(solution)/shard_map/all_gather | solution.py:68
  236.8 21.2 %copy.42 = bf16[32768,2,128]{2,0,1:T(8,128)(2,1)} copy(bf16[32768,2,128]{0,2,1:T(8,128)(2,1)} %bitcast.105) | data formatting | bytes 33554432
  258.1 131.0 %while.11 = (s32[]{:T(128)}, bf16[4,16,2,3,128]{4,1,3,2,0:T(8,128)(2,1)S(1)}, bf16[4,16,2,3,128]{4,1,0,3,2:T(8,128)(2,1)S(1)}, bf16[32768,2,128]{2,0,1:T(8,128)(...) while((s32[]{:T(128)}, ...), condition=%wide.region_6.7_spmd.clone, body=%wide.region_1.6_spmd.clone.sunk | while | flops 1658220288 | bytes 72686784 | solution.py:76
  259.1 12.1 %fusion.83 = (f32[2,16,3]{1,2,0:T(4,128)S(1)}, f32[2,16,3,32768]{3,1,2,0:T(8,128)}) fusion(bf16[32768,2,128]{2,0,1:T(8,128)(2,1)} %get-tuple-element.229, bf16[4,16,2,3,128]{4,1,0,3,2:T(8,128)(2,1)S(1)} %get-tuple-element.228, s32[]{:T(128)} %get-tuple-element.215, pred[32768]{0:T(1024)(128)(4,1)S(1)} %iota_compare_fusion.2), kind=kOutput, calls=%fused_computation.73.clone.1 | convolution fusion | flops 814743424 | bytes 29417860 | tf_op jit(solution)/shard_map/while/body/eval_jaxpr/rkgd,skd->krgs/dot_general | solution.py:33
  271.4 6.5 %fusion.87 = f32[2,16,3]{1,2,0:T(4,128)S(1)} fusion(f32[2,16,3,32768]{3,1,2,0:T(8,128)} %get-tuple-element.200, f32[2,16,3]{1,2,0:T(4,128)S(1)} %max.10), kind=kLoop, calls=%fused_computation.7.clone.1 | loop fusion | flops 6291360 | bytes 12583680 | tf_op jit(solution)/shard_map/while/body/eval_jaxpr/reduce_sum | solution.py:41
  277.9 12.6 %fusion.86 = f32[2,16,3,128]{3,1,2,0:T(8,128)S(1)} fusion(bf16[32768,2,128]{2,0,1:T(8,128)(2,1)} %get-tuple-element.233, f32[2,16,3,32768]{3,1,2,0:T(8,128)} %get-tuple-element.200, f32[2,16,3]{1,2,0:T(4,128)S(1)} %max.10), kind=kOutput, calls=%fused_computation.3.clone.1 | convolution fusion | flops 811597824 | bytes 29409664 | tf_op jit(solution)/shard_map/while/body/eval_jaxpr/krgs,skd->krgd/dot_general | solution.py:42
  291.9 12.1 %fusion.83 = (f32[2,16,3]{1,2,0:T(4,128)S(1)}, f32[2,16,3,32768]{3,1,2,0:T(8,128)}) fusion(bf16[32768,2,128]{2,0,1:T(8,128)(2,1)} %get-tuple-element.229, bf16[4,16,2,3,128]{4,1,0,3,2:T(8,128)(2,1)S(1)} %get-tuple-element.228, s32[]{:T(128)} %get-tuple-element.215, pred[32768]{0:T(1024)(128)(4,1)S(1)} %iota_compare_fusion.2), kind=kOutput, calls=%fused_computation.73.clone.1 | convolution fusion | flops 814743424 | bytes 29417860 | tf_op jit(solution)/shard_map/while/body/eval_jaxpr/rkgd,skd->krgs/dot_general | solution.py:33
  304.2 6.5 %fusion.87 = f32[2,16,3]{1,2,0:T(4,128)S(1)} fusion(f32[2,16,3,32768]{3,1,2,0:T(8,128)} %get-tuple-element.200, f32[2,16,3]{1,2,0:T(4,128)S(1)} %max.10), kind=kLoop, calls=%fused_computation.7.clone.1 | loop fusion | flops 6291360 | bytes 12583680 | tf_op jit(solution)/shard_map/while/body/eval_jaxpr/reduce_sum | solution.py:41
  310.7 12.6 %fusion.86 = f32[2,16,3,128]{3,1,2,0:T(8,128)S(1)} fusion(bf16[32768,2,128]{2,0,1:T(8,128)(2,1)} %get-tuple-element.233, f32[2,16,3,32768]{3,1,2,0:T(8,128)} %get-tuple-element.200, f32[2,16,3]{1,2,0:T(4,128)S(1)} %max.10), kind=kOutput, calls=%fused_computation.3.clone.1 | convolution fusion | flops 811597824 | bytes 29409664 | tf_op jit(solution)/shard_map/while/body/eval_jaxpr/krgs,skd->krgd/dot_general | solution.py:42
  324.6 12.2 %fusion.83 = (f32[2,16,3]{1,2,0:T(4,128)S(1)}, f32[2,16,3,32768]{3,1,2,0:T(8,128)}) fusion(bf16[32768,2,128]{2,0,1:T(8,128)(2,1)} %get-tuple-element.229, bf16[4,16,2,3,128]{4,1,0,3,2:T(8,128)(2,1)S(1)} %get-tuple-element.228, s32[]{:T(128)} %get-tuple-element.215, pred[32768]{0:T(1024)(128)(4,1)S(1)} %iota_compare_fusion.2), kind=kOutput, calls=%fused_computation.73.clone.1 | convolution fusion | flops 814743424 | bytes 29417860 | tf_op jit(solution)/shard_map/while/body/eval_jaxpr/rkgd,skd->krgs/dot_general | solution.py:33
  337.0 6.5 %fusion.87 = f32[2,16,3]{1,2,0:T(4,128)S(1)} fusion(f32[2,16,3,32768]{3,1,2,0:T(8,128)} %get-tuple-element.200, f32[2,16,3]{1,2,0:T(4,128)S(1)} %max.10), kind=kLoop, calls=%fused_computation.7.clone.1 | loop fusion | flops 6291360 | bytes 12583680 | tf_op jit(solution)/shard_map/while/body/eval_jaxpr/reduce_sum | solution.py:41
  343.5 12.6 %fusion.86 = f32[2,16,3,128]{3,1,2,0:T(8,128)S(1)} fusion(bf16[32768,2,128]{2,0,1:T(8,128)(2,1)} %get-tuple-element.233, f32[2,16,3,32768]{3,1,2,0:T(8,128)} %get-tuple-element.200, f32[2,16,3]{1,2,0:T(4,128)S(1)} %max.10), kind=kOutput, calls=%fused_computation.3.clone.1 | convolution fusion | flops 811597824 | bytes 29409664 | tf_op jit(solution)/shard_map/while/body/eval_jaxpr/krgs,skd->krgd/dot_general | solution.py:42
  357.4 12.2 %fusion.83 = (f32[2,16,3]{1,2,0:T(4,128)S(1)}, f32[2,16,3,32768]{3,1,2,0:T(8,128)}) fusion(bf16[32768,2,128]{2,0,1:T(8,128)(2,1)} %get-tuple-element.229, bf16[4,16,2,3,128]{4,1,0,3,2:T(8,128)(2,1)S(1)} %get-tuple-element.228, s32[]{:T(128)} %get-tuple-element.215, pred[32768]{0:T(1024)(128)(4,1)S(1)} %iota_compare_fusion.2), kind=kOutput, calls=%fused_computation.73.clone.1 | convolution fusion | flops 814743424 | bytes 29417860 | tf_op jit(solution)/shard_map/while/body/eval_jaxpr/rkgd,skd->krgs/dot_general | solution.py:33
  369.8 6.5 %fusion.87 = f32[2,16,3]{1,2,0:T(4,128)S(1)} fusion(f32[2,16,3,32768]{3,1,2,0:T(8,128)} %get-tuple-element.200, f32[2,16,3]{1,2,0:T(4,128)S(1)} %max.10), kind=kLoop, calls=%fused_computation.7.clone.1 | loop fusion | flops 6291360 | bytes 12583680 | tf_op jit(solution)/shard_map/while/body/eval_jaxpr/reduce_sum | solution.py:41
  376.3 12.6 %fusion.86 = f32[2,16,3,128]{3,1,2,0:T(8,128)S(1)} fusion(bf16[32768,2,128]{2,0,1:T(8,128)(2,1)} %get-tuple-element.233, f32[2,16,3,32768]{3,1,2,0:T(8,128)} %get-tuple-element.200, f32[2,16,3]{1,2,0:T(4,128)S(1)} %max.10), kind=kOutput, calls=%fused_computation.3.clone.1 | convolution fusion | flops 811597824 | bytes 29409664 | tf_op jit(solution)/shard_map/while/body/eval_jaxpr/krgs,skd->krgd/dot_general | solution.py:42
  389.3 4.2 fusion.53
  393.6 21.3 %reduce-scatter.3.cloned.1.call-done = f32[16,3072]{1,0:T(8,128)} async-done(((f32[64,3072]{1,0:T(8,128)}), f32[16,3072]{1,0:T(8,128)}) %reduce-scatter.3.cloned.1.call-update) | async-done | bytes 196624 | tf_op jit(solution)/shard_map/reduce_scatter | solution.py:78
  416.0 12.8 %all_gather.31 = bf16[64,3072]{1,0:T(8,128)(2,1)S(1)} all-gather(bf16[16,3072]{1,0:T(8,128)(2,1)S(1)} %fusion.44), channel_id=1, replica_groups=mesh['dp'=1,'tp'=4,'cp'=8] {'tp'}, dimensions={0}, use_global_device_ids=true | all-gather | bytes 491520 | tf_op jit(solution)/shard_map/all_gather | solution.py:79
  428.8 7.0 %fusion.54 = f32[64,2048]{1,0:T(8,128)S(1)} fusion(bf16[64,3072]{1,0:T(8,128)(2,1)S(1)} %all_gather.31, bf16[3072,2048]{1,0:T(8,128)(2,1)} %param.27), kind=kOutput, calls=%fused_computation.79 | convolution fusion | flops 805306368 | bytes 13500416 | tf_op jit(solution)/shard_map/dot_general | solution.py:80
  435.8 13.5 %fusion.31 = f32[64,3072]{1,0:T(8,128)} fusion(bf16[2048,3072]{1,0:T(8,128)(2,1)} %param.29, bf16[64,3072]{1,0:T(8,128)(2,1)S(1)} %all_gather.31, bf16[3072,2048]{1,0:T(8,128)(2,1)} %param.28, f32[64,2048]{1,0:T(8,128)S(1)} %fusion.54), kind=kOutput, calls=%fused_computation.39 | convolution fusion | flops 1611399168 | bytes 26869760 | tf_op jit(solution)/shard_map/dot_general | solution.py:83
  449.4 20.1 %reduce-scatter.5.cloned.1.call-done = f32[16,3072]{1,0:T(8,128)} async-done(((f32[64,3072]{1,0:T(8,128)}), f32[16,3072]{1,0:T(8,128)}) %reduce-scatter.5.cloned.1.call-update) | async-done | bytes 196624 | tf_op jit(solution)/shard_map/reduce_scatter | solution.py:84
  (101 shorter events, 29.7 us)
Async XLA Ops:
  6.5 99.9 %copy-start = (bf16[3072,256]{1,0:T(8,128)(2,1)S(1)}, bf16[3072,256]{1,0:T(8,128)(2,1)}, u32[]{:S(2)}) copy-start(bf16[3072,256]{1,0:T(8,128)(2,1)} %param.23) | copy-start | bytes 4718596
  6.6 161.2 %all-gather.3.cloned.1.call-start = ((), (), s32[]{:S(2)}) async-start(), calls=%async_computation.4 | async-start | bytes 18874368 | tf_op jit(solution)/shard_map/all_gather | solution.py:67
  10.6 74.5 %copy-start.10 = (u32[32]{0:T(128)S(1)}, u32[32]{0:T(128)}, u32[]{:S(2)}) copy-start(u32[32]{0:T(128)} %constant.42) | copy-start | bytes 388
  10.6 75.8 %copy-start.8 = (s32[16]{0:T(128)S(1)}, s32[16]{0:T(128)}, u32[]{:S(2)}) copy-start(s32[16]{0:T(128)} %param.17) | copy-start | bytes 196
  10.6 82.8 %copy-start.6 = (bf16[3072]{0:T(1024)(128)(2,1)S(1)}, bf16[3072]{0:T(1024)(128)(2,1)}, u32[]{:S(2)}) copy-start(bf16[3072]{0:T(1024)(128)(2,1)} %param.21) | copy-start | bytes 18436
  10.6 82.8 %copy-start.3 = (bf16[16,3072]{1,0:T(8,128)(2,1)S(1)}, bf16[16,3072]{1,0:T(8,128)(2,1)}, u32[]{:S(2)}) copy-start(bf16[16,3072]{1,0:T(8,128)(2,1)} %param.16) | copy-start | bytes 294916
  47.0 65.3 %copy-start.9 = (u32[32]{0:T(128)S(1)}, u32[32]{0:T(128)}, u32[]{:S(2)}) copy-start(u32[32]{0:T(128)} %constant.47) | copy-start | bytes 388
  47.0 65.8 %copy-start.2 = (bf16[3072,256]{1,0:T(8,128)(2,1)S(1)}, bf16[3072,256]{1,0:T(8,128)(2,1)}, u32[]{:S(2)}) copy-start(bf16[3072,256]{1,0:T(8,128)(2,1)} %param.24) | copy-start | bytes 4718596
  47.0 168.6 %all-gather.5.cloned.1.call-start = ((), (), s32[]{:S(2)}) async-start(), calls=%async_computation.5 | async-start | bytes 18874368 | tf_op jit(solution)/shard_map/all_gather | solution.py:68
  85.1 329.8 %reduce-scatter.3.cloned.1.call-start = ((), (), s32[]{:S(2)}) async-start(), calls=%async_computation.6 | async-start | bytes 983040 | tf_op jit(solution)/shard_map/reduce_scatter | solution.py:78
  236.8 21.2 %copy-start.5 = (bf16[4,16,2,3,128]{4,1,3,2,0:T(8,128)(2,1)S(1)}, bf16[4,16,2,3,128]{4,1,3,2,0:T(8,128)(2,1)}, u32[]{:S(2)}) copy-start(bf16[4,16,2,3,128]{4,1,3,2,0:T(8,128)(2,1)} %custom-call) | copy-start | bytes 294916
  258.1 135.5 %copy-start.7 = (bf16[3072]{0:T(1024)(128)(2,1)S(1)}, bf16[3072]{0:T(1024)(128)(2,1)}, u32[]{:S(2)}) copy-start(bf16[3072]{0:T(1024)(128)(2,1)} %param.26) | copy-start | bytes 18436
  258.1 156.8 %copy-start.4 = (bf16[16,3072]{1,0:T(8,128)(2,1)S(1)}, bf16[16,3072]{1,0:T(8,128)(2,1)}, u32[]{:S(2)}) copy-start(bf16[16,3072]{1,0:T(8,128)(2,1)} %param.16) | copy-start | bytes 294916
  393.5 76.0 %reduce-scatter.5.cloned.1.call-start = ((), (), s32[]{:S(2)}) async-start(), calls=%async_computation.7 | async-start | bytes 983040 | tf_op jit(solution)/shard_map/reduce_scatter | solution.py:84
  428.8 42.3 %copy-start.1 = (bf16[3072,256]{1,0:T(8,128)(2,1)S(1)}, bf16[3072,256]{1,0:T(8,128)(2,1)}, u32[]{:S(2)}) copy-start(bf16[3072,256]{1,0:T(8,128)(2,1)} %param.23) | copy-start | bytes 4718596
Sparse Core Ops, SparseCore 0:
  47.1 81.9 all-gather.2
  130.7 84.9 all-gather.4
  393.6 21.2 reduce-scatter.2
  449.6 19.9 reduce-scatter.4
where the time goes:
time: 481 us; the launch traced here: 478 us
  blocking collectives  148 us (31%)
  matrix products  130 us (27%)
  local copies, waits for them, and re-layouts  104 us (22%)
  waiting for transfers between devices  47.1 us (10%)
  other arithmetic  33.4 us (7%)
  between operations  14.6 us (3%)
    unnamed x32, local copies, waits for them, and re-layouts  52.2 us
    dot_general x4, matrix products, attend_rows(): jnp.einsum('krgs,skd->krgd', cache_probs.astype(jnp.bfloat16), cache_valu...  50.4 us
    dot_general x4, matrix products, attend_rows(): jnp.einsum('rkgd,skd->krgs', block_queries, cache_keys, preferred_element...  48.6 us
    all_to_all x1, blocking collectives, device_layer(): lax.all_to_all(cache_k, 'tp', 1, 0, tiled=True)  32.4 us
    all_to_all x1, blocking collectives, device_layer(): lax.all_to_all(cache_v, 'tp', 1, 0, tiled=True)  29.9 us
    reduce_sum x4, other arithmetic, attend_rows(): jnp.sum(cache_probs, axis=-1, keepdims=True)  25.9 us
    all_gather x1, blocking collectives, device_layer(): new_keys = lax.all_gather(keys_loc, 'cp', axis=0, tiled=True)  22.8 us
    all_gather x1, blocking collectives, device_layer(): new_values = lax.all_gather(values_loc, 'cp', axis=0, tiled=True)  22.2 us
  transfers between devices with their start and end apart: 4, of which 3 were waited for; matrix products, arithmetic and copies ran while one was open for 12% of the time, Pallas kernels for 0%

commit v1 on v0

v1 whole, which is shorter than its diff:
```python
import functools
import math

import jax
import jax.numpy as jnp
from jax import lax
from jax.experimental import pallas as pl
from jax.experimental.pallas import tpu as pltpu
from jax.sharding import PartitionSpec as P

HEAD_DIM = 128
ROPE_BASE = 500000.0
NORM_EPS = 1e-5
HIDDEN = -1e38
SCALE2 = math.log2(math.e) / math.sqrt(HEAD_DIM)
MESH = pl.DeviceIdType.MESH
RING = 4
VMEM_LIMIT = 67_043_328


def place():
    c = lax.axis_index('cp')
    return c // 2, lax.axis_index('tp'), lax.rem(c, 2)


def ring(i):
    return lax.rem(i + RING, RING)


def device(x, y, core):
    return {'tp': ring(y), 'cp': 2 * ring(x) + core}


def remote(src, dst, send_sem, recv_sem, target):
    return pltpu.make_async_remote_copy(src_ref=src, dst_ref=dst, send_sem=send_sem, recv_sem=recv_sem, device_id=target, device_id_type=MESH)


def greet(partners):
    barrier = pltpu.get_barrier_semaphore()
    for partner in partners:
        pl.semaphore_signal(barrier, inc=1, device_id=partner, device_id_type=MESH)
    pl.semaphore_wait(barrier, len(partners))


def normalize(values, gain):
    inv_rms = lax.rsqrt(jnp.mean(values * values, axis=-1, keepdims=True) + NORM_EPS)
    return (values * inv_rms * gain.astype(jnp.float32)).astype(jnp.bfloat16)


def dot(a, b):
    return jnp.dot(a, b, preferred_element_type=jnp.float32)


def dot_nt(a, b):
    return lax.dot_general(a, b, (((1,), (1,)), ((), ())), preferred_element_type=jnp.float32)


def project_kernel(x_ref, gain_ref, wq_hbm, wk_hbm, wv_hbm, cos_ref, sin_ref, q_ref, k_ref, v_ref, wq, wk, wv, rows, load_sem, ss, rs):
    x, y, core = place()
    heads = q_ref.shape[0]
    half = rows.shape[-1] // 2
    loads = []
    for i, (src, dst) in enumerate(((wq_hbm, wq), (wk_hbm, wk), (wv_hbm, wv))):
        width = dst.shape[1]
        loads.append(pltpu.make_async_copy(src.at[:, pl.ds(pl.multiple_of(core * width, width), width)], dst, load_sem.at[i]))
        loads[-1].start()
    sibling, up, down = device(x, y, 1 - core), device(x, y + 1, core), device(x, y - 1, core)
    greet((sibling, up, down))
    rows[core, y] = normalize(x_ref[...].astype(jnp.float32), gain_ref[...])
    lo, hi = pl.ds(0, half), pl.ds(half, half)

    def copy(i, block, cols, target):
        ref = rows.at[core, ring(block)] if cols is None else rows.at[core, ring(block), :, cols]
        return remote(ref, ref, ss.at[i], rs.at[i], target)

    to_up, to_down, own = copy(1, y, None, up), copy(2, y, None, down), copy(0, y, None, sibling)
    to_up.start()
    to_down.start()
    own.start()
    pending = [to_up, to_down, own]

    def go(c):
        c.start()
        pending.append(c)
        return c

    def arrived(i, block, cols):
        ref = rows.at[core, ring(block)] if cols is None else rows.at[core, ring(block), :, cols]
        remote(ref, ref, ss.at[i], rs.at[i], up).wait_recv()

    arrived(1, y - 1, None)
    go(copy(4, y - 1, lo, up))
    go(copy(3, y - 1, None, sibling))
    arrived(2, y + 1, None)
    go(copy(6, y + 1, hi, down))
    go(copy(5, y + 1, None, sibling))
    arrived(4, y - 2, lo)
    go(copy(7, y - 2, lo, sibling))
    arrived(6, y + 2, hi)
    go(copy(8, y + 2, hi, sibling))
    other = 1 - core

    def from_sibling(i, block, cols):
        ref = rows.at[other, ring(block)] if cols is None else rows.at[other, ring(block), :, cols]
        remote(ref, ref, ss.at[i], rs.at[i], sibling).wait_recv()

    from_sibling(0, y, None)
    from_sibling(3, y - 1, None)
    from_sibling(5, y + 1, None)
    from_sibling(7, y - 2, lo)
    from_sibling(8, y + 2, hi)
    for load in loads:
        load.wait()
    a = rows[...].reshape(-1, rows.shape[-1])
    cos, sin = cos_ref[...], sin_ref[...]

    def rotate(p):
        return (p * cos + pltpu.roll(p, HEAD_DIM // 2, axis=1) * sin).astype(jnp.bfloat16)

    q = dot(a, wq[...])
    for g in range(heads):
        q_ref[g] = rotate(q[:, g * HEAD_DIM : (g + 1) * HEAD_DIM])
    k_ref[...] = rotate(dot(a, wk[...]))
    v_ref[...] = dot(a, wv[...]).astype(jnp.bfloat16)
    for c in pending:
        c.wait_send()


def project(hidden, gain, w_query, w_key, w_value, cos, sin):
    shard_rows, width = hidden.shape
    kv_local = w_key.shape[1] // HEAD_DIM
    heads = w_query.shape[1] // w_key.shape[1]
    rows = 2 * RING * shard_rows
    assert kv_local == 2
    vmem, hbm = pl.BlockSpec(memory_space=pltpu.VMEM), pl.BlockSpec(memory_space=pl.ANY)
    return pl.pallas_call(
        project_kernel,
        out_shape=[
            jax.ShapeDtypeStruct((heads, rows, HEAD_DIM), jnp.bfloat16),
            jax.ShapeDtypeStruct((rows, HEAD_DIM), jnp.bfloat16),
            jax.ShapeDtypeStruct((rows, HEAD_DIM), jnp.bfloat16),
        ],
        in_specs=[vmem, vmem, hbm, hbm, hbm, vmem, vmem],
        out_specs=[vmem] * 3,
        scratch_shapes=[
            pltpu.VMEM((width, heads * HEAD_DIM), jnp.bfloat16),
            pltpu.VMEM((width, HEAD_DIM), jnp.bfloat16),
            pltpu.VMEM((width, HEAD_DIM), jnp.bfloat16),
            pltpu.VMEM((2, RING, shard_rows, width), jnp.bfloat16),
            pltpu.SemaphoreType.DMA((3,)),
            pltpu.SemaphoreType.DMA((9,)),
            pltpu.SemaphoreType.DMA((9,)),
        ],
        compiler_params=pltpu.CompilerParams(collective_id=0, has_side_effects=True, vmem_limit_bytes=VMEM_LIMIT),
    )(hidden, gain, w_query, w_key, w_value, cos, sin)


def merge(parts):
    top = parts[0][HEAD_DIM : HEAD_DIM + 1]
    for p in parts[1:]:
        top = jnp.maximum(top, p[HEAD_DIM : HEAD_DIM + 1])
    total, norm = 0.0, 0.0
    for p in parts:
        weight = jnp.exp2(p[HEAD_DIM : HEAD_DIM + 1] - top)
        total = total + p[:HEAD_DIM] * weight
        norm = norm + p[HEAD_DIM + 1 : HEAD_DIM + 2] * weight
    return total, top, norm


def put_block(ref, index, total, top, norm):
    ref[(*index, pl.ds(0, HEAD_DIM))] = total
    ref[(*index, pl.ds(HEAD_DIM, 8))] = jnp.concatenate([top, norm, jnp.zeros((6, total.shape[1]), jnp.float32)], axis=0)


def attend_kernel(len_ref, q_in, kn_in, vn_in, ck_hbm, cv_hbm, o_ref, kbuf, vbuf, vt, qbuf, bias, cbias, sbuf, ob, r1, n1, r2, n2, ox, oin, csem, xs, xr, gs, gr, ps, pr, os_, or_):
    x, y, core = place()
    heads = q_in.shape[0]
    slots = ck_hbm.shape[0]
    cached = 2 * slots
    rows = q_in.shape[1]
    half_rows = rows // (4 * RING)
    other = 1 - core
    a1, a2 = x + core * (y - x), y + core * (x - y)
    sibling = device(x, y, other)

    def on1(d):
        return device(x + d * other, y + d * core, core)

    def on2(d):
        return device(x + d * core, y + d * other, core)

    local, cross = [], []
    mine = pl.ds(pl.multiple_of(core * slots, slots), slots)
    for j in range(RING):
        for i, (src, dst) in enumerate(((ck_hbm, kbuf), (cv_hbm, vbuf))):
            cols = pl.ds(pl.multiple_of((2 * j + core) * HEAD_DIM, HEAD_DIM), HEAD_DIM)
            local.append(pltpu.make_async_copy(src.at[:, cols], dst.at[j, mine], csem.at[2 * j + i]))
            local[-1].start()
    greet((sibling, on1(1), on1(-1), on2(1), on2(-1)))

    for g in range(heads):
        qbuf[g, a2, a1] = q_in[g]

    def q1(g, i, block, part, target):
        ref = qbuf.at[g, a2, ring(block)] if part is None else qbuf.at[g, a2, ring(block), part]
        return remote(ref, ref, gs.at[g, i], gr.at[g, i], target)

    def q2(g, i, block, part, target):
        ref = qbuf.at[g, ring(block)] if part is None else qbuf.at[g, ring(block), part]
        return remote(ref, ref, gs.at[g, i], gr.at[g, i], target)

    lo, hi = pl.ds(0, rows // 2), pl.ds(rows // 2, rows // 2)
    two_lo, two_hi = pl.ds(0, 2), pl.ds(2, 2)
    for g in range(heads):
        q1(g, 0, a1, None, on1(1)).start()
        q1(g, 1, a1, None, on1(-1)).start()
    for j in range(RING):
        for i, (src, dst) in enumerate(((ck_hbm, kbuf), (cv_hbm, vbuf))):
            cols = pl.ds(pl.multiple_of((2 * j + other) * HEAD_DIM, HEAD_DIM), HEAD_DIM)
            cross.append(remote(src.at[:, cols], dst.at[j, mine], xs.at[2 * j + i], xr.at[2 * j + i], sibling))
            cross[-1].start()

    def q1_relay(g):
        q1(g, 0, a1 - 1, None, on1(1)).wait_recv()
        q1(g, 2, a1 - 1, lo, on1(1)).start()
        q1(g, 1, a1 + 1, None, on1(1)).wait_recv()
        q1(g, 3, a1 + 1, hi, on1(-1)).start()

    def q1_done(g):
        q1(g, 2, a1 - 2, lo, on1(1)).wait_recv()
        q1(g, 3, a1 + 2, hi, on1(1)).wait_recv()
        q2(g, 4, a2, None, on2(1)).start()
        q2(g, 5, a2, None, on2(-1)).start()

    def q2_relay(g):
        q2(g, 4, a2 - 1, None, on2(1)).wait_recv()
        q2(g, 6, a2 - 1, two_lo, on2(1)).start()
        q2(g, 5, a2 + 1, None, on2(1)).wait_recv()
        q2(g, 7, a2 + 1, two_hi, on2(-1)).start()

    def q2_done(g):
        q2(g, 6, a2 - 2, two_lo, on2(1)).wait_recv()
        q2(g, 7, a2 + 2, two_hi, on2(1)).wait_recv()

    for g in range(heads):
        q1_relay(g)
    for g in range(heads):
        q1_done(g)

    tail = pl.ds(cached, rows)
    for j in range(RING):
        keep = jnp.where(y == j, 1.0, 0.0).astype(jnp.bfloat16)
        kbuf[j, tail] = kn_in[...] * keep
        vbuf[j, tail] = vn_in[...] * keep
    length = len_ref[0]
    for part in range(2):
        base = ((2 * x + part) * RING + y) * slots
        slot = base + lax.broadcasted_iota(jnp.int32, (slots, HEAD_DIM), 0)
        bias[pl.ds(part * slots, slots)] = jnp.where(slot < length, 0.0, HIDDEN)

    def order(i, xg):
        c_part, rest = i // (rows // 2), lax.rem(i, rows // 2)
        t_part, r = rest // (2 * half_rows), lax.rem(rest, 2 * half_rows)
        owner = (2 * xg + c_part) * RING + t_part
        run = jnp.where(r < half_rows, owner, 4 * RING * RING - 1 - owner)
        return run * half_rows + lax.rem(r, half_rows)

    key_order = order(lax.broadcasted_iota(jnp.int32, (rows, rows), 0), x)
    for xg in range(RING):
        query_order = order(lax.broadcasted_iota(jnp.int32, (rows, rows), 1), xg)
        cbias[xg] = jnp.where(key_order <= query_order, 0.0, HIDDEN)
    for c in local:
        c.wait()
    for c in cross:
        c.wait_recv()
    block = 512
    for j in range(RING):
        for b in range(cached // block):
            vt[j, :, pl.ds(b * block, block)] = vbuf[j, pl.ds(b * block, block)].T
        vt[j, :, tail] = vbuf[j, tail].T

    def p1(g, i, src, dst, target):
        return remote(src, dst, ps.at[g, i], pr.at[g, i], target)

    def send_a(g):
        far, near_up, near_down = ring(a1 + 2), ring(a1 + 1), ring(a1 - 1)
        return (
            p1(g, 0, ob.at[g, far, two_lo], r1.at[g, 0], on1(1)),
            p1(g, 1, ob.at[g, far, two_hi], r1.at[g, 1], on1(-1)),
            p1(g, 2, ob.at[g, near_up, two_hi], n1.at[g, 0, two_hi], on1(1)),
            p1(g, 3, ob.at[g, near_down, two_lo], n1.at[g, 1, two_lo], on1(-1)),
            p1(g, 4, ob.at[g, near_up, two_lo], n1.at[g, 0, two_lo], on1(1)),
            p1(g, 5, ob.at[g, near_down, two_hi], n1.at[g, 1, two_hi], on1(-1)),
        )

    def send_b(g):
        d = 1 - 2 * lax.rem(g, 2)
        return (
            p1(g, 6, ob.at[g, a1, ring(a2 + 2)], r2.at[g], on2(d)),
            p1(g, 7, ob.at[g, a1, ring(a2 - d)], n2.at[g, 0], on2(-d)),
            p1(g, 8, ob.at[g, a1, ring(a2 + d)], n2.at[g, 1], on2(d)),
        )

    def reduce_start(g):
        for c in send_a(g)[:4]:
            c.start()

    def reduce_1(g):
        copies = send_a(g)
        for i in range(2):
            copies[i].wait_recv()
            to = ring(a1 + 1 - 2 * i)
            for b in range(2):
                put_block(ob, (g, to, 2 * i + b), *merge([ob[g, to, 2 * i + b], r1[g, i, b]]))
            copies[4 + i].start()

    def reduce_2(g):
        copies = send_a(g)
        for i in range(2, 6):
            copies[i].wait_recv()
        for b in range(RING):
            put_block(ob, (g, a1, b), *merge([ob[g, a1, b], n1[g, 0, b], n1[g, 1, b]]))
        copies = send_b(g)
        copies[0].start()
        copies[1].start()

    def reduce_3(g):
        copies = send_b(g)
        copies[0].wait_recv()
        to = ring(a2 + 1 - 2 * lax.rem(g, 2))
        put_block(ob, (g, a1, to), *merge([ob[g, a1, to], r2[g]]))
        copies[2].start()

    def reduce_4(g):
        copies = send_b(g)
        copies[1].wait_recv()
        copies[2].wait_recv()
        total, _, norm = merge([ob[g, a1, a2], n2[g, 0], n2[g, 1]])
        ox[g] = (total / norm).T.astype(jnp.bfloat16)

    q2_relay(0)

    @pl.loop(0, heads * 2 * RING)
    def _(u):
        g, t, part = u // (2 * RING), lax.rem(u // 2, RING), lax.rem(u, 2)

        @pl.when(lax.rem(u, 2 * RING) == 0)
        def _():
            q2_done(g)

        places = []
        for i in range(2):
            xg = 2 * part + i
            places.append((xg + core * (t - xg), t + core * (xg - t)))
        q = jnp.concatenate([qbuf[g, p2, p1_] for p1_, p2 in places], axis=0)
        top = None
        for b in range(cached // block):
            at = pl.ds(b * block, block)
            mask = bias[at]
            s = dot_nt(kbuf[t, at], q) + jnp.concatenate([mask, mask], axis=1)
            sbuf[at] = s
            here = jnp.max(s, axis=0, keepdims=True)
            top = here if top is None else jnp.maximum(top, here)
        unseen = jnp.where(t == y, 0.0, HIDDEN)
        s = dot_nt(kbuf[t, tail], q) + jnp.concatenate([cbias[2 * part], cbias[2 * part + 1]], axis=1) + unseen
        sbuf[tail] = s
        top = jnp.maximum(top, jnp.max(s, axis=0, keepdims=True)) * SCALE2
        norm, total = 0.0, 0.0
        for at in [pl.ds(b * block, block) for b in range(cached // block)] + [tail]:
            e = jnp.exp2(sbuf[at] * SCALE2 - top)
            norm = norm + jnp.sum(e, axis=0, keepdims=True)
            total = total + dot(vt[t, :, at], e.astype(jnp.bfloat16))
        for i, (p1_, p2) in enumerate(places):
            cut = slice(i * rows, (i + 1) * rows)
            put_block(ob, (g, p1_, p2), total[:, cut], top[:, cut], norm[:, cut])

        r = lax.rem(u, 2 * RING)
        for g_next in range(1, heads):
            @pl.when(u == 2 * g_next)
            def _():
                q2_relay(g_next)

        @pl.when(r == 2 * RING - 1)
        def _():
            reduce_start(g)

        for at, step in ((2, reduce_1), (4, reduce_2), (5, reduce_3), (6, reduce_4)):
            @pl.when(jnp.logical_and(r == at, g > 0))
            def _():
                step(g - 1)

    for step in (reduce_1, reduce_2, reduce_3, reduce_4):
        step(heads - 1)

    keep = pl.ds(pl.multiple_of(core * (rows // 2), rows // 2), rows // 2)
    give = pl.ds(pl.multiple_of(other * (rows // 2), rows // 2), rows // 2)
    swap = remote(ox.at[:, give], oin, os_, or_, sibling)
    swap.start()
    o_ref[core] = ox[:, keep]
    swap.wait()
    o_ref[other] = oin[...]
    for c in cross:
        c.wait_send()
    for g in range(heads):
        for c in (q1(g, 0, a1, None, on1(1)), q1(g, 1, a1, None, on1(1)), q1(g, 2, a1, lo, on1(1)), q1(g, 3, a1, hi, on1(1))):
            c.wait_send()
        for c in (q2(g, 4, a2, None, on2(1)), q2(g, 5, a2, None, on2(1)), q2(g, 6, a2, two_lo, on2(1)), q2(g, 7, a2, two_hi, on2(1))):
            c.wait_send()
        for c in (*send_a(g), *send_b(g)):
            c.wait_send()


def attend(cache_len, q, k_new, v_new, cache_k, cache_v):
    heads, rows, _ = q.shape
    slots = cache_k.shape[0]
    total = 2 * slots + rows
    bf16, f32 = jnp.bfloat16, jnp.float32
    deep = HEAD_DIM + 8
    vmem, hbm, smem = pl.BlockSpec(memory_space=pltpu.VMEM), pl.BlockSpec(memory_space=pl.ANY), pl.BlockSpec(memory_space=pltpu.SMEM)
    dma = pltpu.SemaphoreType.DMA
    return pl.pallas_call(
        attend_kernel,
        out_shape=jax.ShapeDtypeStruct((2, heads, rows // 2, HEAD_DIM), bf16),
        in_specs=[smem, vmem, vmem, vmem, hbm, hbm],
        out_specs=vmem,
        scratch_shapes=[
            pltpu.VMEM((RING, total, HEAD_DIM), bf16),
            pltpu.VMEM((RING, total, HEAD_DIM), bf16),
            pltpu.VMEM((RING, HEAD_DIM, total), bf16),
            pltpu.VMEM((heads, RING, RING, rows, HEAD_DIM), bf16),
            pltpu.VMEM((2 * slots, HEAD_DIM), f32),
            pltpu.VMEM((RING, rows, rows), f32),
            pltpu.VMEM((total, 2 * rows), f32),
            pltpu.VMEM((heads, RING, RING, deep, rows), f32),
            pltpu.VMEM((heads, 2, 2, deep, rows), f32),
            pltpu.VMEM((heads, 2, RING, deep, rows), f32),
            pltpu.VMEM((heads, deep, rows), f32),
            pltpu.VMEM((heads, 2, deep, rows), f32),
            pltpu.VMEM((heads, rows, HEAD_DIM), bf16),
            pltpu.VMEM((heads, rows // 2, HEAD_DIM), bf16),
            dma((2 * RING,)),
            dma((2 * RING,)),
            dma((2 * RING,)),
            dma((heads, 8)),
            dma((heads, 8)),
            dma((heads, 9)),
            dma((heads, 9)),
            dma,
            dma,
        ],
        compiler_params=pltpu.CompilerParams(collective_id=1, has_side_effects=True, vmem_limit_bytes=VMEM_LIMIT),
    )(cache_len, q, k_new, v_new, cache_k, cache_v)


def mlp_kernel(o_in, x_ref, gain_ref, wo_hbm, wg_hbm, wu_hbm, wd_hbm, out_ref, wo, wg, wu, wd, part, far, near, mid, rows, act, wsem, ss, rs):
    x, y, core = place()
    shard_rows, width = x_ref.shape
    all_rows = RING * shard_rows
    half = width // 2
    loads = [pltpu.make_async_copy(src, dst, wsem.at[i]) for i, (src, dst) in enumerate(((wo_hbm, wo), (wg_hbm, wg), (wu_hbm, wu), (wd_hbm, wd)))]
    for load in loads:
        load.start()
    up, down = device(x, y + 1, core), device(x, y - 1, core)
    greet((up, down))
    lo, hi = pl.ds(0, half), pl.ds(half, half)
    pending = []

    def reduce_rows(n):
        def copy(i, src, dst, target):
            return remote(src, dst, ss.at[n, i], rs.at[n, i], target)

        copies = (
            copy(0, part.at[ring(y + 2), :, lo], far.at[n, 0], up),
            copy(1, part.at[ring(y + 2), :, hi], far.at[n, 1], down),
            copy(2, part.at[ring(y + 1), :, hi], near.at[n, 0, :, hi], up),
            copy(3, part.at[ring(y - 1), :, lo], near.at[n, 1, :, lo], down),
            copy(4, part.at[ring(y + 1), :, lo], near.at[n, 0, :, lo], up),
            copy(5, part.at[ring(y - 1), :, hi], near.at[n, 1, :, hi], down),
        )
        for c in copies[:4]:
            c.start()
        copies[0].wait_recv()
        part[ring(y + 1), :, lo] = part[ring(y + 1), :, lo] + far[n, 0]
        copies[4].start()
        copies[1].wait_recv()
        part[ring(y - 1), :, hi] = part[ring(y - 1), :, hi] + far[n, 1]
        copies[5].start()
        for c in copies[2:]:
            c.wait_recv()
        total = part[y] + (near[n, 0] + near[n, 1])
        for c in copies:
            c.wait_send()
        return total

    o = jnp.concatenate([o_in[c, g] for c in range(2) for g in range(o_in.shape[1])], axis=1)
    loads[0].wait()
    cols = 768

    @pl.loop(0, width // cols)
    def _(i):
        at = pl.ds(pl.multiple_of(i * cols, cols), cols)
        part[:, :, at] = dot(o, wo[:, at]).reshape(RING, shard_rows, cols)

    h = (x_ref[...].astype(jnp.float32) + reduce_rows(0)).astype(jnp.bfloat16)
    mid[...] = h
    rows[y] = normalize(h.astype(jnp.float32), gain_ref[...])

    def copy(i, block, cut, target):
        ref = rows.at[ring(block)] if cut is None else rows.at[ring(block), :, cut]
        return remote(ref, ref, ss.at[2, i], rs.at[2, i], target)

    sends = [copy(0, y, None, up), copy(1, y, None, down)]
    for c in sends:
        c.start()
    copy(0, y - 1, None, up).wait_recv()
    sends.append(copy(2, y - 1, lo, up))
    sends[-1].start()
    copy(1, y + 1, None, up).wait_recv()
    sends.append(copy(3, y + 1, hi, down))
    sends[-1].start()
    copy(2, y - 2, lo, up).wait_recv()
    copy(3, y + 2, hi, up).wait_recv()
    b = rows[...].reshape(all_rows, width)
    loads[1].wait()
    loads[2].wait()
    wide = 512

    @pl.loop(0, act.shape[1] // wide)
    def _(i):
        at = pl.ds(pl.multiple_of(i * wide, wide), wide)
        gate = dot(b, wg[:, at])
        act[:, at] = (gate * jax.nn.sigmoid(gate) * dot(b, wu[:, at])).astype(jnp.bfloat16)

    loads[3].wait()
    a = act[...]

    @pl.loop(0, width // cols)
    def _(i):
        at = pl.ds(pl.multiple_of(i * cols, cols), cols)
        part[:, :, at] = dot(a, wd[:, at]).reshape(RING, shard_rows, cols)

    out_ref[...] = (mid[...].astype(jnp.float32) + reduce_rows(1)).astype(jnp.bfloat16)
    for c in sends:
        c.wait_send()


def mlp(o, hidden, gain, w_out, w_gate, w_up, w_down):
    shard_rows, width = hidden.shape
    inner = w_gate.shape[1]
    bf16, f32 = jnp.bfloat16, jnp.float32
    vmem, hbm = pl.BlockSpec(memory_space=pltpu.VMEM), pl.BlockSpec(memory_space=pl.ANY)
    dma = pltpu.SemaphoreType.DMA
    return pl.pallas_call(
        mlp_kernel,
        out_shape=jax.ShapeDtypeStruct(hidden.shape, bf16),
        in_specs=[vmem, vmem, vmem, hbm, hbm, hbm, hbm],
        out_specs=vmem,
        scratch_shapes=[
            pltpu.VMEM(w_out.shape, bf16),
            pltpu.VMEM(w_gate.shape, bf16),
            pltpu.VMEM(w_up.shape, bf16),
            pltpu.VMEM(w_down.shape, bf16),
            pltpu.VMEM((RING, shard_rows, width), f32),
            pltpu.VMEM((2, 2, shard_rows, width // 2), f32),
            pltpu.VMEM((2, 2, shard_rows, width), f32),
            pltpu.VMEM((shard_rows, width), bf16),
            pltpu.VMEM((RING, shard_rows, width), bf16),
            pltpu.VMEM((RING * shard_rows, inner), bf16),
            dma((4,)),
            dma((3, 6)),
            dma((3, 6)),
        ],
        compiler_params=pltpu.CompilerParams(collective_id=2, has_side_effects=True, vmem_limit_bytes=VMEM_LIMIT),
    )(o, hidden, gain, w_out, w_gate, w_up, w_down)


def solution(mesh):
    devices = mesh.shape['tp'] * mesh.shape['cp']
    assert mesh.shape['tp'] == RING and mesh.shape['cp'] == 2 * RING
    token_spec = P(('dp', 'cp', 'tp'), None)
    column_spec = P(None, 'tp')
    row_spec = P('tp', None)

    def tables(cache_len, shard_rows):
        half_rows, half_dim = shard_rows // 2, HEAD_DIM // 2
        row = jnp.arange(2 * RING * shard_rows, dtype=jnp.int32)
        owner = (lax.axis_index('cp') // 2) * (2 * RING) + row // shard_rows
        r = row % shard_rows
        run = jnp.where(r < half_rows, owner, 2 * devices - 1 - owner)
        pos = cache_len[0] + run * half_rows + r % half_rows
        inv_freq = 1.0 / (ROPE_BASE ** (jnp.arange(half_dim, dtype=jnp.float32) * (2.0 / HEAD_DIM)))
        angles = pos.astype(jnp.float32)[:, None] * inv_freq[None, :]
        cos, sin = jnp.cos(angles), jnp.sin(angles)
        return jnp.concatenate([cos, cos], axis=1), jnp.concatenate([-sin, sin], axis=1)

    def device_layer(hidden, pos, cache_len, cache_k, cache_v, norm1_gain, w_query, w_key, w_value, w_out, norm2_gain, w_gate, w_up, w_down):
        cos, sin = tables(cache_len, hidden.shape[0])
        q, k_new, v_new = project(hidden, norm1_gain[None], w_query, w_key, w_value, cos, sin)
        o = attend(cache_len, q, k_new, v_new, cache_k, cache_v)
        return mlp(o, hidden, norm2_gain[None], w_out, w_gate, w_up, w_down)

    return jax.shard_map(device_layer, mesh=mesh, in_specs=(token_spec, P(('dp', 'cp', 'tp')), P('dp'), token_spec, token_spec, P(), column_spec, column_spec, column_spec, row_spec, P(), column_spec, column_spec, row_spec), out_specs=token_spec, check_vma=False)
```

time: 481 us -> 148 us (0.31)
  blocking collectives: 148 us -> 0 us
  Pallas kernels: 0 us -> 141 us
  matrix products: 130 us -> 0 us
  local copies, waits for them, and re-layouts: 104 us -> 4.13 us
  waiting for transfers between devices: 47.1 us -> 0 us
  other arithmetic: 33.4 us -> 1.09 us
  between operations: 14.6 us -> 0.69 us
    pallas_call x0 -> x3, Pallas kernels: none -> 141 us  [the longest x1 87.3 us: attend(): pl.pallas_call(attend_kernel, out_shape=jax.ShapeDtypeStruct((2, heads, r...]
    dot_general x22 -> x0, matrix products: 130 us -> none  [the longest x4 50.4 us: attend_rows(): jnp.einsum('krgs,skd->krgd', cache_probs.astype(jnp.bfloat16), cache_valu...]
    all_gather x4 -> x0, blocking collectives: 70.6 us -> none  [the longest x1 22.8 us: device_layer(): new_keys = lax.all_gather(keys_loc, 'cp', axis=0, tiled=True)]
    all_to_all x2 -> x0, blocking collectives: 62.3 us -> none  [the longest x1 32.4 us: device_layer(): lax.all_to_all(cache_k, 'tp', 1, 0, tiled=True)]
    unnamed x32 -> x1, local copies, waits for them, and re-layouts: 52.2 us -> 1.54 us
    all_gather x2 -> x0, local copies, waits for them, and re-layouts: 42.4 us -> none  [the longest x1 21.2 us: device_layer(): lax.all_gather(lax.all_to_all(cache_k, 'tp', 1, 0, tiled=True), 'cp', axi...]
    reduce_scatter x2 -> x0, waiting for transfers between devices: 41.4 us -> none  [the longest x1 21.3 us: device_layer(): lax.psum_scatter(attn_part, 'tp', scatter_dimension=0, tiled=True)]
    reduce_sum x10 -> x0, other arithmetic: 27.9 us -> none  [the longest x4 25.9 us: attend_rows(): jnp.sum(cache_probs, axis=-1, keepdims=True)]
  transfers between devices with their start and end apart: 4 -> 0, of which waited for: 3 -> 0; matrix products, arithmetic and copies ran while one was open for 12% -> 0% of each run, Pallas kernels for 0% -> 0%
where the time goes in v1:
time: 148 us; the launch traced here: 147 us
  Pallas kernels  141 us (95%)
  local copies, waits for them, and re-layouts  4.13 us (3%)
    pallas_call x1, Pallas kernels, attend(): pl.pallas_call(attend_kernel, out_shape=jax.ShapeDtypeStruct((2, heads, r...  87.3 us
    pallas_call x1, Pallas kernels, mlp(): pl.pallas_call(mlp_kernel, out_shape=jax.ShapeDtypeStruct(hidden.shape, b...  39.7 us
    pallas_call x1, Pallas kernels, project(): pl.pallas_call(project_kernel, out_shape=[jax.ShapeDtypeStruct((heads, ro...  14.5 us

profile of v1, /device:TPU:98, one launch (start us, length us, event | category | flops | bytes accessed | tf_op | source)
XLA Modules:
  0.0 147.4 jit_solution(11262237015806640875)
XLA Ops:
  0.7 0.3 fusion
  1.0 0.8 pad_maximum_fusion
  1.8 1.3 broadcast_in_dim.8.gain_ref
  3.1 14.5 %shard_map.127 = (bf16[3,128,128]{2,1,0:T(8,128)(2,1)}, bf16[128,128]{1,0:T(8,128)(2,1)}, bf16[128,128]{1,0:T(8,128)(2,1)}) custom-call(bf16[16,3072]{1,0:T(8,128)(2,1)} %x_ref.3, bf16[1,3072]{1,0:T(2,128)(2,1)} %broadcast_in_dim.8.gain_ref, bf16[3072,768]{1,0:T(8,128)(2,1)} %wq_hbm.1, bf16[3072,256]{1,0:T(8,128)(2,1)} %wk_hbm.1, bf16[3072,256]{1,0:T(8,128)(2,1)} %wv_hbm.1, ...), custom_call_target="tpu_custom_call" | custom-call | tf_op jit(solution)/shard_map/pallas_call | solution.py:136
  17.5 87.3 %shard_map.128.o_in = bf16[2,3,64,128]{3,2,1,0:T(8,128)(2,1)} custom-call(s32[1]{0:T(128)} %copy.15.len_ref, bf16[3,128,128]{2,1,0:T(8,128)(2,1)} %get-tuple-element.8.q_in, bf16[128,128]{1,0:T(8,128)(2,1)} %get-tuple-element.9.kn_in, bf16[128,128]{1,0:T(8,128)(2,1)} %get-tuple-element.10.vn_in, bf16[1024,1024]{1,0:T(8,128)(2,1)} %ck_hbm.1, ...), custom_call_target="tpu_custom_call" | custom-call | tf_op jit(solution)/shard_map/pallas_call | solution.py:421
  104.8 1.3 broadcast_in_dim.9.gain_ref
  106.1 39.7 %shard_map.129 = bf16[16,3072]{1,0:T(8,128)(2,1)} custom-call(bf16[2,3,64,128]{3,2,1,0:T(8,128)(2,1)} %shard_map.128.o_in, bf16[16,3072]{1,0:T(8,128)(2,1)} %x_ref.3, bf16[1,3072]{1,0:T(2,128)(2,1)} %broadcast_in_dim.9.gain_ref, bf16[768,3072]{1,0:T(8,128)(2,1)} %wo_hbm.1, bf16[3072,2048]{1,0:T(8,128)(2,1)} %wg_hbm.1, bf16[3072,2048]{1,0:T(8,128)(2,1)} %wu_hbm.1, ...), custom_call_target="tpu_custom_call" | custom-call | tf_op jit(solution)/shard_map/pallas_call | solution.py:553
  145.9 1.5 %copy.16 = bf16[16,3072]{1,0:T(8,128)(2,1)} copy(bf16[16,3072]{1,0:T(8,128)(2,1)} %shard_map.129) | data formatting | bytes 196608
  (2 shorter events, 0.0 us)

commit v2 on v0

v2 whole, which is shorter than its diff:
```python
import functools
import math

import jax
import jax.numpy as jnp
from jax import lax
from jax.experimental import pallas as pl
from jax.experimental.pallas import tpu as pltpu
from jax.sharding import PartitionSpec as P

HEAD_DIM = 128
ROPE_BASE = 500000.0
NORM_EPS = 1e-5
HIDDEN = -1e38
SCALE2 = math.log2(math.e) / math.sqrt(HEAD_DIM)
MESH = pl.DeviceIdType.MESH
RING = 4
VMEM_LIMIT = 67_043_328


def place():
    c = lax.axis_index('cp')
    return c // 2, lax.axis_index('tp'), lax.rem(c, 2)


def ring(i):
    return lax.rem(i + RING, RING)


def device(x, y, core):
    return {'tp': ring(y), 'cp': 2 * ring(x) + core}


def remote(src, dst, send_sem, recv_sem, target):
    return pltpu.make_async_remote_copy(src_ref=src, dst_ref=dst, send_sem=send_sem, recv_sem=recv_sem, device_id=target, device_id_type=MESH)


def greet(partners):
    for partner in partners:
        pl.semaphore_signal(pltpu.get_barrier_semaphore(), inc=1, device_id=partner, device_id_type=MESH)


def normalize(values, gain):
    inv_rms = lax.rsqrt(jnp.mean(values * values, axis=-1, keepdims=True) + NORM_EPS)
    return (values * inv_rms * gain.astype(jnp.float32)).astype(jnp.bfloat16)


def dot(a, b):
    return jnp.dot(a, b, preferred_element_type=jnp.float32)


def dot_nt(a, b):
    return lax.dot_general(a, b, (((1,), (1,)), ((), ())), preferred_element_type=jnp.float32)


def merge(parts):
    top = parts[0][HEAD_DIM : HEAD_DIM + 1]
    for p in parts[1:]:
        top = jnp.maximum(top, p[HEAD_DIM : HEAD_DIM + 1])
    total, norm = 0.0, 0.0
    for p in parts:
        weight = jnp.exp2(p[HEAD_DIM : HEAD_DIM + 1] - top)
        total = total + p[:HEAD_DIM] * weight
        norm = norm + p[HEAD_DIM + 1 : HEAD_DIM + 2] * weight
    return total, top, norm


def put_block(ref, index, total, top, norm):
    ref[(*index, pl.ds(0, HEAD_DIM))] = total
    ref[(*index, pl.ds(HEAD_DIM, 8))] = jnp.concatenate([top, norm, jnp.zeros((6, total.shape[1]), jnp.float32)], axis=0)


def layer_kernel(
    len_ref, x_ref, gain1_ref, gain2_ref, cos_ref, sin_ref, ck_hbm, cv_hbm, wq_hbm, wk_hbm, wv_hbm, wo_hbm, wg_hbm, wu_hbm, wd_hbm, out_ref,
    a_rows, knew, vnew, vt, qbuf, bias, cbias, ob, r1, n1, r2, n2, ox, oin, obuf, sbuf_a, sbuf_b, top_a, top_b, wo, wg, wu, wd, part, far, near, mid, b_rows, act,
    load_sem, csem, xs, xr, as_, ar, fs, fr, bs, br, gs, gr, ps, pr, ts, tr, os_, or_, wsem, ss, rs,
):
    x, y, core = place()
    other = 1 - core
    shard_rows, width = x_ref.shape
    heads = qbuf.shape[0]
    slots = ck_hbm.shape[0]
    cached = 2 * slots
    rows = qbuf.shape[3]
    half_rows = shard_rows // 2
    half = width // 2
    tail = pl.ds(cached, rows)
    lo, hi = pl.ds(0, half), pl.ds(half, half)
    a1, a2 = x + core * (y - x), y + core * (x - y)
    sibling, up, down = device(x, y, other), device(x, y + 1, core), device(x, y - 1, core)

    def on1(d):
        return device(x + d * other, y + d * core, core)

    def on2(d):
        return device(x + d * core, y + d * other, core)

    mine = pl.ds(pl.multiple_of(core * slots, slots), slots)

    def head_cols(j, c):
        return pl.ds(pl.multiple_of((2 * j + c) * HEAD_DIM, HEAD_DIM), HEAD_DIM)

    def kept(j, i):
        return wd.at[mine, pl.ds((RING * (1 - i) + j) * HEAD_DIM, HEAD_DIM)]

    local = [pltpu.make_async_copy(src.at[:, head_cols(j, core)], kept(j, i), csem.at[2 * j + i]) for j in range(RING) for i, src in enumerate((ck_hbm, cv_hbm))]
    cross = [remote(src.at[:, head_cols(j, other)], kept(j, i), xs.at[2 * j + i], xr.at[2 * j + i], sibling) for j in range(RING) for i, src in enumerate((ck_hbm, cv_hbm))]
    weights = [pltpu.make_async_copy(src, dst, wsem.at[i]) for i, (src, dst) in enumerate(((wo_hbm, wo), (wg_hbm, wg), (wu_hbm, wu)))]

    def order(i, xg):
        c_part, rest = i // (rows // 2), lax.rem(i, rows // 2)
        t_part, r = rest // shard_rows, lax.rem(rest, shard_rows)
        owner = (2 * xg + c_part) * RING + t_part
        run = jnp.where(r < half_rows, owner, 4 * RING * RING - 1 - owner)
        return run * half_rows + lax.rem(r, half_rows)

    def masks():
        length = len_ref[0]
        for piece in range(2):
            base = ((2 * x + piece) * RING + y) * slots
            slot = base + lax.broadcasted_iota(jnp.int32, (slots, HEAD_DIM), 0)
            lane = lax.broadcasted_iota(jnp.int32, (slots, HEAD_DIM), 1)
            bias[pl.ds(piece * slots, slots)] = jnp.where(jnp.logical_and(slot >= length, lane == 0), HIDDEN, 0.0).astype(jnp.bfloat16)
        key_order = order(lax.broadcasted_iota(jnp.int32, (rows, rows), 0), x)
        for xg in range(RING):
            query_order = order(lax.broadcasted_iota(jnp.int32, (rows, rows), 1), xg)
            cbias[xg] = jnp.where(key_order <= query_order, 0.0, HIDDEN)

    two_lo, two_hi = pl.ds(0, 2), pl.ds(2, 2)

    def q1(g):
        ref = qbuf.at[g, a2, a1]
        return [remote(ref, ref, gs.at[g, i], gr.at[g, i], on1(d)) for i, d in enumerate((2, 1, -1))]

    def q2(g, i):
        d, index, piece, to = ((0, 0, two_lo, 1), (1, 0, two_hi, -1), (2, 0, two_hi, 1), (3, 0, two_lo, -1), (4, -1, two_lo, 1), (5, 1, two_hi, -1))[i]
        ref = qbuf.at[g, ring(a2 + index), piece]
        return remote(ref, ref, gs.at[g, 3 + i], gr.at[g, 3 + i], on2(to))

    def q1_done(g):
        for c in q1(g):
            c.wait_recv()
        for i in range(4):
            q2(g, i).start()

    def q2_relay(g):
        for i in range(2):
            q2(g, i).wait_recv()
            q2(g, 4 + i).start()

    def q2_early(g):
        q2(g, 3).wait_recv()

    def q2_late(g):
        for i in (2, 4, 5):
            q2(g, i).wait_recv()

    pending = []

    def go(c):
        c.start()
        pending.append(c)
        return c

    block = 512

    def turn(j):
        for b in range(cached // block):
            vt[j, :, pl.ds(b * block, block)] = wd[pl.ds(b * block, block), pl.ds(j * HEAD_DIM, HEAD_DIM)].T

    def gather(block, sends, recvs, seen):
        hops = ((0, lo, up), (0, hi, down), (0, hi, up), (0, lo, down), (-1, lo, up), (1, hi, down))
        arrivals = ((-1, lo), (1, hi), (-1, hi), (1, lo), (-2, lo), (2, hi))

        def hop(n):
            d, cols, to = hops[n]
            return remote(block(y + d, cols), block(y + d, cols), sends.at[n], recvs.at[n], to)

        for n in range(4):
            go(hop(n))
        for n, (d, cols) in enumerate(arrivals):
            hop(n).wait_recv()
            if n < 2:
                go(hop(4 + n))
            seen(n, block(y + d, cols), cols)

    loads = []
    wide = heads * HEAD_DIM
    for i, (src, w, at) in enumerate(((wq_hbm, wide, 0), (wk_hbm, HEAD_DIM, wide), (wv_hbm, HEAD_DIM, wide + HEAD_DIM))):
        loads.append(pltpu.make_async_copy(src.at[:, pl.ds(pl.multiple_of(core * w, w), w)], wg.at[:, pl.ds(at, w)], load_sem.at[i]))
        loads[-1].start()
    for c in local:
        c.start()
    partners = (sibling, on1(1), on1(-1), on2(1), on2(-1), on1(2))
    greet(partners)
    a_rows[core, y] = normalize(x_ref[...].astype(jnp.float32), gain1_ref[...].reshape(1, width))
    pl.semaphore_wait(pltpu.get_barrier_semaphore(), len(partners))
    whole = pl.ds(0, width)

    def row_block(c):
        return lambda i, cols: a_rows.at[c, ring(i), :, cols]

    def forward(n, block, cols):
        go(remote(block, block, fs.at[n], fr.at[n], sibling))

    own = row_block(core)(y, whole)
    go(remote(own, own, fs.at[6], fr.at[6], sibling))
    for c in cross:
        c.start()
    gather(row_block(core), as_, ar, forward)
    for n, (d, cols) in enumerate(((-1, lo), (1, hi), (-1, hi), (1, lo), (-2, lo), (2, hi), (0, whole))):
        ref = row_block(other)(y + d, cols)
        remote(ref, ref, fs.at[n], fr.at[n], sibling).wait_recv()
    for load in loads:
        load.wait()
    a = a_rows[...].reshape(rows, width)
    cos, sin = cos_ref[...], sin_ref[...]

    def rotate(p):
        return (p * cos + pltpu.roll(p, HEAD_DIM // 2, axis=1) * sin).astype(jnp.bfloat16)

    q = dot(a, wg[:, :wide])
    for g in range(heads):
        qbuf[g, a2, a1] = rotate(q[:, g * HEAD_DIM : (g + 1) * HEAD_DIM])
        for c in q1(g):
            c.start()
    knew[...] = rotate(dot(a, wg[:, wide : wide + HEAD_DIM]))
    vnew[...] = dot(a, wg[:, wide + HEAD_DIM : wide + 2 * HEAD_DIM]).T.astype(jnp.bfloat16)
    for w in weights:
        w.start()
    masks()
    for i in range(2 * RING):
        local[i].wait()
        cross[i].wait_recv()
    turn(0)
    for g in range(heads):
        q1_done(g)
    for j in range(1, RING):
        turn(j)

    def granule(g, h):
        flip = (g + 1) // heads
        back = h + flip - 2 * flip * h
        return ring(a2 - back), ring(a2 + 1 + back)

    def first(g, h):
        far, near_up, near_down = ring(a1 + 2), ring(a1 + 1), ring(a1 - 1)
        even, odd = granule(g, h)

        def hop(i, src, dst, target):
            return remote(src, dst, ps.at[g, h, i], pr.at[g, h, i], target)

        return (
            lambda: hop(0, ob.at[g, far, even], r1.at[g, h, 0], on1(1)),
            lambda: hop(1, ob.at[g, far, odd], r1.at[g, h, 1], on1(-1)),
            lambda: hop(2, ob.at[g, near_up, odd], n1.at[g, 0, odd], on1(1)),
            lambda: hop(3, ob.at[g, near_down, even], n1.at[g, 1, even], on1(-1)),
            lambda: hop(4, ob.at[g, near_up, even], n1.at[g, 0, even], on1(1)),
            lambda: hop(5, ob.at[g, near_down, odd], n1.at[g, 1, odd], on1(-1)),
        )

    def second(g):
        d = 1 - 2 * lax.rem(g, 2)

        def hop(i, src, dst, target):
            return remote(src, dst, ts.at[g, i], tr.at[g, i], target)

        return (
            lambda: hop(0, ob.at[g, a1, ring(a2 + 2)], r2.at[g], on2(d)),
            lambda: hop(1, ob.at[g, a1, ring(a2 - d)], n2.at[g, 0], on2(-d)),
            lambda: hop(2, ob.at[g, a1, ring(a2 + d)], n2.at[g, 1], on2(d)),
        )

    def reduce_0(g, h):
        for c in first(g, h)[:4]:
            c().start()

    def reduce_1(g, h):
        copies = first(g, h)
        for i, b in enumerate(granule(g, h)):
            copies[i]().wait_recv()
            to = ring(a1 + 1 - 2 * i)
            put_block(ob, (g, to, b), *merge([ob[g, to, b], r1[g, h, i]]))
            copies[4 + i]().start()

    def reduce_2(g, h):
        copies = first(g, h)
        for i in range(2, 6):
            copies[i]().wait_recv()
        for b in granule(g, h):
            put_block(ob, (g, a1, b), *merge([ob[g, a1, b], n1[g, 0, b], n1[g, 1, b]]))

    def reduce_3(g):
        copies = second(g)
        copies[0]().start()
        copies[1]().start()

    def reduce_4(g):
        copies = second(g)
        copies[0]().wait_recv()
        to = ring(a2 + 1 - 2 * lax.rem(g, 2))
        put_block(ob, (g, a1, to), *merge([ob[g, a1, to], r2[g]]))
        copies[2]().start()

    def reduce_5(g):
        copies = second(g)
        copies[1]().wait_recv()
        copies[2]().wait_recv()
        total, _, norm = merge([ob[g, a1, a2], n2[g, 0], n2[g, 1]])
        ox[g] = (total / norm).T.astype(jnp.bfloat16)

    def unit(u):
        g, h, i = u // 8, lax.rem(u // 4, 2), lax.rem(u, 4)
        near, far_off = granule(g, h)
        t = (near + (i // 2) * (far_off - near)) * other + i * core
        pair = [(2 * lax.rem(i, 2) + n) * other + (near, far_off)[n] * core for n in range(2)]
        places = [(g, xg + core * (t - xg), t + core * (xg - t)) for xg in pair]
        return t, pair, places

    step = 512
    chunks = [pl.ds(b * step, step) for b in range(cached // step)] + [tail]

    def keys_at(t):
        return pl.ds(pl.multiple_of((RING + t) * HEAD_DIM, HEAD_DIM), HEAD_DIM)

    def advance(ahead, s_out, top_out, u, s_in, top_in):
        if ahead is not None:
            t_next, pair, q_places = unit(ahead)
            q = jnp.concatenate([qbuf[g, p2, p1] for g, p1, p2 in q_places], axis=0)
            unit_col = jnp.where(lax.broadcasted_iota(jnp.int32, q.shape, 1) == 0, 1.0, 0.0).astype(jnp.bfloat16)
            deep_q = jnp.concatenate([q, unit_col], axis=1)
            unseen = jnp.where(t_next == y, 0.0, HIDDEN)
            peak = jnp.full((8, 2 * rows), -jnp.inf, jnp.float32)
        if u is not None:
            t, _, places = unit(u)
            top = top_in[...]
            norm, total = jnp.zeros((8, 2 * rows), jnp.float32), 0.0
        for at in chunks:
            if ahead is not None:
                if at is tail:
                    s = dot_nt(knew[...], q) + (jnp.concatenate([cbias[xg] for xg in pair], axis=1) + unseen)
                else:
                    s = dot_nt(jnp.concatenate([wd[at, keys_at(t_next)], bias[at]], axis=1), deep_q)
                s_out[at] = s
                peak = jnp.maximum(peak, jnp.max(s.reshape(-1, 8, 2 * rows), axis=0))
            if u is not None:
                e = jnp.exp2(s_in[at] * SCALE2 - top)
                norm = norm + jnp.sum(e.reshape(-1, 8, 2 * rows), axis=0)
                total = total + dot(vnew[...] if at is tail else vt[t, :, at], e.astype(jnp.bfloat16))
        if ahead is not None:
            top_out[...] = jnp.max(peak, axis=0, keepdims=True) * SCALE2
        if u is not None:
            norm = jnp.sum(norm, axis=0, keepdims=True)
            for n, index in enumerate(places):
                cut = slice(n * rows, (n + 1) * rows)
                put_block(ob, index, total[:, cut], top[:, cut], norm[:, cut])

    q2_relay(0)
    q2_early(0)
    units = heads * 8
    advance(0, sbuf_a, top_a, None, None, None)

    @pl.loop(0, units // 2)
    def _(i):
        @pl.when(i == 1)
        def _():
            q2_late(0)

        for g in range(1, heads):
            @pl.when(i == 4 * g - 1)
            def _():
                q2_early(g)
                q2_late(g)

        u = 2 * i
        advance(u + 1, sbuf_b, top_b, u, sbuf_a, top_a)
        advance(jnp.minimum(u + 2, units - 1), sbuf_a, top_a, u + 1, sbuf_b, top_b)

        for g in range(1, heads):
            @pl.when(i == g - 1)
            def _():
                q2_relay(g)

        n = i // 2
        late = lax.rem(i, 2) == 1

        @pl.when(late)
        def _():
            reduce_0(n // 2, lax.rem(n, 2))

        @pl.when(jnp.logical_and(late, n >= 1))
        def _():
            reduce_1((n - 1) // 2, lax.rem(n - 1, 2))

        @pl.when(jnp.logical_and(late, n >= 2))
        def _():
            reduce_2((n - 2) // 2, lax.rem(n - 2, 2))

        for at, g, stage in [(4 * g + 7, g, reduce_3) for g in range(heads)] + [(4 * g + 9, g, reduce_4) for g in range(heads)] + [(4 * g + 11, g, reduce_5) for g in range(heads)]:
            if at < units // 2:
                @pl.when(i == at)
                def _():
                    stage(g)

    cols = width // RING

    sent = []

    def settle():
        while sent:
            sent.pop().wait_send()

    def reduce_rows(n, product):
        quarter = [pl.ds(i * cols, cols) for i in range(RING)]
        near_up, near_down = ring(y + 1), ring(y - 1)

        def hop(i, src, dst, target):
            return remote(src, dst, ss.at[n, i], rs.at[n, i], target)

        a_hops = [hop(i, part.at[ring(y + 2), :, q], far.at[n, :, q], up if i < 2 else down) for i, q in enumerate(quarter)]
        b_hops = [hop(4, part.at[near_up, :, hi], near.at[n, 0, :, hi], up), hop(5, part.at[near_down, :, lo], near.at[n, 1, :, lo], down)]
        c_hops = [hop(6 + i, part.at[near_up if i < 2 else near_down, :, q], near.at[n, i // 2, :, q], up if i < 2 else down) for i, q in enumerate(quarter)]
        turns = (0, 2, 1, 3)
        for i in turns:
            part[:, :, quarter[i]] = product(quarter[i]).reshape(RING, shard_rows, cols)
            a_hops[i].start()
        for c in b_hops:
            c.start()
        for i in turns:
            a_hops[i].wait_recv()
            to = near_up if i < 2 else near_down
            part[to, :, quarter[i]] = part[to, :, quarter[i]] + far[n, :, quarter[i]]
            c_hops[i].start()
        for c in b_hops + c_hops:
            c.wait_recv()
        sent.extend(a_hops + b_hops + c_hops)
        return part[y] + (near[n, 0] + near[n, 1])

    down_load = pltpu.make_async_copy(wd_hbm, wd, wsem.at[3])
    down_load.start()
    last = heads - 1
    reduce_1(last, 1)
    reduce_2(last, 0)
    reduce_3(last)
    reduce_4(last - 1)
    reduce_2(last, 1)
    reduce_4(last)
    reduce_5(last - 1)
    reduce_5(last)

    keep = pl.ds(pl.multiple_of(core * (rows // 2), rows // 2), rows // 2)
    give = pl.ds(pl.multiple_of(other * (rows // 2), rows // 2), rows // 2)
    swap = remote(ox.at[:, give], oin, os_, or_, sibling)
    swap.start()
    obuf[core] = ox[:, keep]
    swap.wait()
    obuf[other] = oin[...]
    o = jnp.concatenate([obuf[c, g] for c in range(2) for g in range(heads)], axis=1)
    weights[0].wait()
    h = (x_ref[...].astype(jnp.float32) + reduce_rows(0, lambda at: dot(o, wo[:, at]))).astype(jnp.bfloat16)
    mid[...] = h
    b_rows[y] = normalize(h.astype(jnp.float32), gain2_ref[...].reshape(1, width))

    gather(lambda i, cut: b_rows.at[ring(i), :, cut], bs, br, lambda *_: None)
    b = b_rows[...].reshape(RING * shard_rows, width)
    weights[1].wait()
    weights[2].wait()
    wide = act.shape[1] // 2

    @pl.loop(0, act.shape[1] // wide)
    def _(i):
        at = pl.ds(pl.multiple_of(i * wide, wide), wide)
        gate = dot(b, wg[:, at])
        act[:, at] = (gate * jax.nn.sigmoid(gate) * dot(b, wu[:, at])).astype(jnp.bfloat16)

    down_load.wait()
    inner = act[...]

    settle()
    out_ref[...] = (mid[...].astype(jnp.float32) + reduce_rows(1, lambda at: dot(inner, wd[:, at]))).astype(jnp.bfloat16)
    settle()
    for c in pending + cross:
        c.wait_send()
    for g in range(heads):
        for c in q1(g) + [q2(g, i) for i in range(6)]:
            c.wait_send()
        for c in (*first(g, 0), *first(g, 1), *second(g)):
            c().wait_send()


def layer(cache_len, hidden, gain1, gain2, cos, sin, cache_k, cache_v, w_query, w_key, w_value, w_out, w_gate, w_up, w_down):
    shard_rows, width = hidden.shape
    kv_local = w_key.shape[1] // HEAD_DIM
    heads = w_query.shape[1] // w_key.shape[1]
    rows = 2 * RING * shard_rows
    slots = cache_k.shape[0]
    total = 2 * slots + rows
    inner = w_gate.shape[1]
    deep = HEAD_DIM + 8
    assert kv_local == 2 and w_down.shape[0] >= 2 * slots and width >= 2 * RING * HEAD_DIM and inner >= (heads + 2) * HEAD_DIM and cache_k.shape[1] == 2 * RING * HEAD_DIM
    bf16, f32 = jnp.bfloat16, jnp.float32
    vmem, hbm, smem = pl.BlockSpec(memory_space=pltpu.VMEM), pl.BlockSpec(memory_space=pl.ANY), pl.BlockSpec(memory_space=pltpu.SMEM)
    dma = pltpu.SemaphoreType.DMA
    return pl.pallas_call(
        layer_kernel,
        out_shape=jax.ShapeDtypeStruct(hidden.shape, bf16),
        in_specs=[smem] + [vmem] * 5 + [hbm] * 9,
        out_specs=vmem,
        scratch_shapes=[
            pltpu.VMEM((2, RING, shard_rows, width), bf16),
            pltpu.VMEM((rows, HEAD_DIM), bf16),
            pltpu.VMEM((HEAD_DIM, rows), bf16),
            pltpu.VMEM((RING, HEAD_DIM, 2 * slots), bf16),
            pltpu.VMEM((heads, RING, RING, rows, HEAD_DIM), bf16),
            pltpu.VMEM((2 * slots, HEAD_DIM), bf16),
            pltpu.VMEM((RING, rows, rows), f32),
            pltpu.VMEM((heads, RING, RING, deep, rows), f32),
            pltpu.VMEM((heads, 2, 2, deep, rows), f32),
            pltpu.VMEM((heads, 2, RING, deep, rows), f32),
            pltpu.VMEM((heads, deep, rows), f32),
            pltpu.VMEM((heads, 2, deep, rows), f32),
            pltpu.VMEM((heads, rows, HEAD_DIM), bf16),
            pltpu.VMEM((heads, rows // 2, HEAD_DIM), bf16),
            pltpu.VMEM((2, heads, rows // 2, HEAD_DIM), bf16),
            pltpu.VMEM((total, 2 * rows), f32),
            pltpu.VMEM((total, 2 * rows), f32),
            pltpu.VMEM((1, 2 * rows), f32),
            pltpu.VMEM((1, 2 * rows), f32),
            pltpu.VMEM(w_out.shape, bf16),
            pltpu.VMEM(w_gate.shape, bf16),
            pltpu.VMEM(w_up.shape, bf16),
            pltpu.VMEM(w_down.shape, bf16),
            pltpu.VMEM((RING, shard_rows, width), f32),
            pltpu.VMEM((2, shard_rows, width), f32),
            pltpu.VMEM((2, 2, shard_rows, width), f32),
            pltpu.VMEM((shard_rows, width), bf16),
            pltpu.VMEM((RING, shard_rows, width), bf16),
            pltpu.VMEM((RING * shard_rows, inner), bf16),
            dma((3,)),
            dma((2 * RING,)),
            *(dma(shape) for shape in ((2 * RING,), (6,), (7,), (6,), (heads, 9), (heads, 2, 6), (heads, 3)) for _ in range(2)),
            dma,
            dma,
            dma((4,)),
            dma((2, 10)),
            dma((2, 10)),
        ],
        compiler_params=pltpu.CompilerParams(collective_id=0, has_side_effects=True, vmem_limit_bytes=VMEM_LIMIT),
        name='attend',
    )(cache_len, hidden, gain1, gain2, cos, sin, cache_k, cache_v, w_query, w_key, w_value, w_out, w_gate, w_up, w_down)


def solution(mesh):
    devices = mesh.shape['tp'] * mesh.shape['cp']
    assert mesh.shape['tp'] == RING and mesh.shape['cp'] == 2 * RING
    token_spec = P(('dp', 'cp', 'tp'), None)
    column_spec = P(None, 'tp')
    row_spec = P('tp', None)

    def tables(cache_len, shard_rows):
        half_rows, half_dim = shard_rows // 2, HEAD_DIM // 2
        row = jnp.arange(2 * RING * shard_rows, dtype=jnp.int32)
        owner = (lax.axis_index('cp') // 2) * (2 * RING) + row // shard_rows
        r = row % shard_rows
        run = jnp.where(r < half_rows, owner, 2 * devices - 1 - owner)
        pos = cache_len[0] + run * half_rows + r % half_rows
        inv_freq = 1.0 / (ROPE_BASE ** (jnp.arange(half_dim, dtype=jnp.float32) * (2.0 / HEAD_DIM)))
        angles = pos.astype(jnp.float32)[:, None] * inv_freq[None, :]
        cos, sin = jnp.cos(angles), jnp.sin(angles)
        return jnp.concatenate([cos, cos], axis=1), jnp.concatenate([-sin, sin], axis=1)

    def device_layer(hidden, pos, cache_len, cache_k, cache_v, norm1_gain, w_query, w_key, w_value, w_out, norm2_gain, w_gate, w_up, w_down):
        cos, sin = tables(cache_len, hidden.shape[0])
        return layer(cache_len, hidden, norm1_gain, norm2_gain, cos, sin, cache_k, cache_v, w_query, w_key, w_value, w_out, w_gate, w_up, w_down)

    return jax.shard_map(device_layer, mesh=mesh, in_specs=(token_spec, P(('dp', 'cp', 'tp')), P('dp'), token_spec, token_spec, P(), column_spec, column_spec, column_spec, row_spec, P(), column_spec, column_spec, row_spec), out_specs=token_spec, check_vma=False)
```

time: 481 us -> 101 us (0.21)
  blocking collectives: 148 us -> 0 us
  matrix products: 130 us -> 0 us
  local copies, waits for them, and re-layouts: 104 us -> 1.54 us
  Pallas kernels: 0 us -> 96.4 us
  waiting for transfers between devices: 47.1 us -> 0 us
  other arithmetic: 33.4 us -> 1.08 us
  between operations: 14.6 us -> 0.68 us
    dot_general x22 -> x0, matrix products: 130 us -> none  [the longest x4 50.4 us: attend_rows(): jnp.einsum('krgs,skd->krgd', cache_probs.astype(jnp.bfloat16), cache_valu...]
    pallas_call x0 -> x1, Pallas kernels: none -> 96.4 us  [layer(): pl.pallas_call(layer_kernel, out_shape=jax.ShapeDtypeStruct(hidden.shape,...]
    all_gather x4 -> x0, blocking collectives: 70.6 us -> none  [the longest x1 22.8 us: device_layer(): new_keys = lax.all_gather(keys_loc, 'cp', axis=0, tiled=True)]
    all_to_all x2 -> x0, blocking collectives: 62.3 us -> none  [the longest x1 32.4 us: device_layer(): lax.all_to_all(cache_k, 'tp', 1, 0, tiled=True)]
    unnamed x32 -> x1, local copies, waits for them, and re-layouts: 52.2 us -> 1.54 us
    all_gather x2 -> x0, local copies, waits for them, and re-layouts: 42.4 us -> none  [the longest x1 21.2 us: device_layer(): lax.all_gather(lax.all_to_all(cache_k, 'tp', 1, 0, tiled=True), 'cp', axi...]
    reduce_scatter x2 -> x0, waiting for transfers between devices: 41.4 us -> none  [the longest x1 21.3 us: device_layer(): lax.psum_scatter(attn_part, 'tp', scatter_dimension=0, tiled=True)]
    reduce_sum x10 -> x0, other arithmetic: 27.9 us -> none  [the longest x4 25.9 us: attend_rows(): jnp.sum(cache_probs, axis=-1, keepdims=True)]
  transfers between devices with their start and end apart: 4 -> 0, of which waited for: 3 -> 0; matrix products, arithmetic and copies ran while one was open for 12% -> 0% of each run, Pallas kernels for 0% -> 0%
where the time goes in v2:
time: 101 us; the launch traced here: 99.7 us
  Pallas kernels  96.4 us (95%)
  local copies, waits for them, and re-layouts  1.54 us (2%)
  other arithmetic  1.08 us (1%)
    pallas_call x1, Pallas kernels, layer(): pl.pallas_call(layer_kernel, out_shape=jax.ShapeDtypeStruct(hidden.shape,...  96.4 us

profile of v2, /device:TPU:98, one launch (start us, length us, event | category | flops | bytes accessed | tf_op | source)
XLA Modules:
  0.0 99.7 jit_solution(8476471851179562232)
XLA Ops:
  0.7 0.3 fusion
  1.0 0.7 pad_maximum_fusion
  1.7 96.4 %attend.1 = bf16[16,3072]{1,0:T(8,128)(2,1)} custom-call(s32[1]{0:T(128)} %copy.15.len_ref, bf16[16,3072]{1,0:T(8,128)(2,1)} %x_ref.1, bf16[3072]{0:T(1024)(128)(2,1)} %gain1_ref.1, bf16[3072]{0:T(1024)(128)(2,1)} %gain2_ref.1, f32[128,128]{1,0:T(8,128)} %get-tuple-element.8.cos_ref, f32[128,128]{1,0:T(8,128)} %get-tuple-element.9.sin_ref, ...), custom_call_target="tpu_custom_call" | custom-call | tf_op jit(solution)/shard_map/attend/pallas_call | solution.py:504
  98.1 1.5 %copy.16 = bf16[16,3072]{1,0:T(8,128)(2,1)} copy(bf16[16,3072]{1,0:T(8,128)(2,1)} %attend.1) | data formatting | bytes 196608
  (2 shorter events, 0.0 us)

commit v3 on v2

--- a/solution.py
+++ b/solution.py
@@ -191,7 +191,7 @@
         loads[-1].start()
     for c in local:
         c.start()
-    partners = (sibling, on1(1), on1(-1), on2(1), on2(-1), on1(2))
+    partners = (sibling, *(on(d) for on in (on1, on2) for d in (1, -1, 2)))
     greet(partners)
     a_rows[core, y] = normalize(x_ref[...].astype(jnp.float32), gain1_ref[...].reshape(1, width))
     pl.semaphore_wait(pltpu.get_barrier_semaphore(), len(partners))
@@ -202,11 +202,12 @@
 
     def forward(n, block, cols):
         go(remote(block, block, fs.at[n], fr.at[n], sibling))
+        if n == 1:
+            for c in cross:
+                c.start()
 
     own = row_block(core)(y, whole)
     go(remote(own, own, fs.at[6], fr.at[6], sibling))
-    for c in cross:
-        c.start()
     gather(row_block(core), as_, ar, forward)
     for n, (d, cols) in enumerate(((-1, lo), (1, hi), (-1, hi), (1, lo), (-2, lo), (2, hi), (0, whole))):
         ref = row_block(other)(y + d, cols)
@@ -238,12 +239,14 @@
     for j in range(1, RING):
         turn(j)
 
+    def back(g, h):
+        flip = (g + 1) // heads
+        return h + flip - 2 * flip * h
+
     def granule(g, h):
-        flip = (g + 1) // heads
-        back = h + flip - 2 * flip * h
-        return ring(a2 - back), ring(a2 + 1 + back)
-
-    def first(g, h):
+        return ring(a2 - back(g, h)), ring(a2 + 1 + back(g, h))
+
+    def first(g, h, straight=False):
         far, near_up, near_down = ring(a1 + 2), ring(a1 + 1), ring(a1 - 1)
         even, odd = granule(g, h)
 
@@ -251,8 +254,8 @@
             return remote(src, dst, ps.at[g, h, i], pr.at[g, h, i], target)
 
         return (
-            lambda: hop(0, ob.at[g, far, even], r1.at[g, h, 0], on1(1)),
-            lambda: hop(1, ob.at[g, far, odd], r1.at[g, h, 1], on1(-1)),
+            lambda: hop(0, ob.at[g, far, even], r1.at[g, h, 0], on1(2 if straight else 1)),
+            lambda: hop(1, ob.at[g, far, odd], r1.at[g, h, 1], on1(2 if straight else -1)),
             lambda: hop(2, ob.at[g, near_up, odd], n1.at[g, 0, odd], on1(1)),
             lambda: hop(3, ob.at[g, near_down, even], n1.at[g, 1, even], on1(-1)),
             lambda: hop(4, ob.at[g, near_up, even], n1.at[g, 0, even], on1(1)),
@@ -260,19 +263,18 @@
         )
 
     def second(g):
-        d = 1 - 2 * lax.rem(g, 2)
-
-        def hop(i, src, dst, target):
-            return remote(src, dst, ts.at[g, i], tr.at[g, i], target)
-
-        return (
-            lambda: hop(0, ob.at[g, a1, ring(a2 + 2)], r2.at[g], on2(d)),
-            lambda: hop(1, ob.at[g, a1, ring(a2 - d)], n2.at[g, 0], on2(-d)),
-            lambda: hop(2, ob.at[g, a1, ring(a2 + d)], n2.at[g, 1], on2(d)),
-        )
-
-    def reduce_0(g, h):
-        for c in first(g, h)[:4]:
+        def hop(i, d, dst):
+            return lambda: remote(ob.at[g, a1, ring(a2 + d)], dst, ts.at[g, i], tr.at[g, i], on2(d))
+
+        return hop(0, 2, r2.at[g]), hop(1, -1, n2.at[g, 0]), hop(2, 1, n2.at[g, 1])
+
+    def swap(g):
+        give = pl.ds(pl.multiple_of(other * (rows // 2), rows // 2), rows // 2)
+        return remote(ox.at[g, give], oin.at[g], os_.at[g], or_.at[g], sibling)
+
+    def reduce_0(g, h, straight):
+        copies = first(g, h, straight)
+        for c in copies if straight else copies[:4]:
             c().start()
 
     def reduce_1(g, h):
@@ -283,31 +285,27 @@
             put_block(ob, (g, to, b), *merge([ob[g, to, b], r1[g, h, i]]))
             copies[4 + i]().start()
 
-    def reduce_2(g, h):
-        copies = first(g, h)
-        for i in range(2, 6):
-            copies[i]().wait_recv()
-        for b in granule(g, h):
-            put_block(ob, (g, a1, b), *merge([ob[g, a1, b], n1[g, 0, b], n1[g, 1, b]]))
+    def reduce_2(g, h, straight=False):
+        for c in first(g, h)[0 if straight else 2 :]:
+            c().wait_recv()
+        for i, b in enumerate(granule(g, h)):
+            put_block(ob, (g, a1, b), *merge([ob[g, a1, b], n1[g, 0, b], n1[g, 1, b]] + ([r1[g, h, i]] if straight else [])))
+
+        @pl.when(back(g, h) == 0)
+        def _():
+            second(g)[2]().start()
+
+        @pl.when(back(g, h) == 1)
+        def _():
+            second(g)[0]().start()
+            second(g)[1]().start()
 
     def reduce_3(g):
-        copies = second(g)
-        copies[0]().start()
-        copies[1]().start()
-
-    def reduce_4(g):
-        copies = second(g)
-        copies[0]().wait_recv()
-        to = ring(a2 + 1 - 2 * lax.rem(g, 2))
-        put_block(ob, (g, a1, to), *merge([ob[g, a1, to], r2[g]]))
-        copies[2]().start()
-
-    def reduce_5(g):
-        copies = second(g)
-        copies[1]().wait_recv()
-        copies[2]().wait_recv()
-        total, _, norm = merge([ob[g, a1, a2], n2[g, 0], n2[g, 1]])
+        for c in second(g):
+            c().wait_recv()
+        total, _, norm = merge([ob[g, a1, a2], n2[g, 0], n2[g, 1], r2[g]])
         ox[g] = (total / norm).T.astype(jnp.bfloat16)
+        swap(g).start()
 
     def unit(u):
         g, h, i = u // 8, lax.rem(u // 4, 2), lax.rem(u, 4)
@@ -384,9 +382,13 @@
         n = i // 2
         late = lax.rem(i, 2) == 1
 
-        @pl.when(late)
-        def _():
-            reduce_0(n // 2, lax.rem(n, 2))
+        @pl.when(jnp.logical_and(late, n < 2 * heads - 1))
+        def _():
+            reduce_0(n // 2, lax.rem(n, 2), False)
+
+        @pl.when(jnp.logical_and(late, n == 2 * heads - 1))
+        def _():
+            reduce_0(heads - 1, 1, True)
 
         @pl.when(jnp.logical_and(late, n >= 1))
         def _():
@@ -396,14 +398,11 @@
         def _():
             reduce_2((n - 2) // 2, lax.rem(n - 2, 2))
 
-        for at, g, stage in [(4 * g + 7, g, reduce_3) for g in range(heads)] + [(4 * g + 9, g, reduce_4) for g in range(heads)] + [(4 * g + 11, g, reduce_5) for g in range(heads)]:
-            if at < units // 2:
-                @pl.when(i == at)
-                def _():
-                    stage(g)
+        @pl.when(i == units // 2 - 1)
+        def _():
+            reduce_3(0)
 
     cols = width // RING
-
     sent = []
 
     def settle():
@@ -439,21 +438,15 @@
     down_load = pltpu.make_async_copy(wd_hbm, wd, wsem.at[3])
     down_load.start()
     last = heads - 1
-    reduce_1(last, 1)
     reduce_2(last, 0)
+    for g in range(1, last):
+        reduce_3(g)
+    reduce_2(last, 1, True)
     reduce_3(last)
-    reduce_4(last - 1)
-    reduce_2(last, 1)
-    reduce_4(last)
-    reduce_5(last - 1)
-    reduce_5(last)
-
     keep = pl.ds(pl.multiple_of(core * (rows // 2), rows // 2), rows // 2)
-    give = pl.ds(pl.multiple_of(other * (rows // 2), rows // 2), rows // 2)
-    swap = remote(ox.at[:, give], oin, os_, or_, sibling)
-    swap.start()
     obuf[core] = ox[:, keep]
-    swap.wait()
+    for g in range(heads):
+        swap(g).wait_recv()
     obuf[other] = oin[...]
     o = jnp.concatenate([obuf[c, g] for c in range(2) for g in range(heads)], axis=1)
     weights[0].wait()
@@ -486,6 +479,7 @@
             c.wait_send()
         for c in (*first(g, 0), *first(g, 1), *second(g)):
             c().wait_send()
+        swap(g).wait_send()
 
 
 def layer(cache_len, hidden, gain1, gain2, cos, sin, cache_k, cache_v, w_query, w_key, w_value, w_out, w_gate, w_up, w_down):
@@ -538,9 +532,7 @@
             pltpu.VMEM((RING * shard_rows, inner), bf16),
             dma((3,)),
             dma((2 * RING,)),
-            *(dma(shape) for shape in ((2 * RING,), (6,), (7,), (6,), (heads, 9), (heads, 2, 6), (heads, 3)) for _ in range(2)),
-            dma,
-            dma,
+            *(dma(shape) for shape in ((2 * RING,), (6,), (7,), (6,), (heads, 9), (heads, 2, 6), (heads, 3), (heads,)) for _ in range(2)),
             dma((4,)),
             dma((2, 10)),
             dma((2, 10)),

time: 101 us -> 100 us (0.990)
  no operation moved by 1% of the time
where the time goes in v3:
time: 100 us; the launch traced here: 99 us
  Pallas kernels  95.7 us (96%)
  local copies, waits for them, and re-layouts  1.54 us (2%)
  other arithmetic  1.08 us (1%)
    pallas_call x1, Pallas kernels, layer(): pl.pallas_call(layer_kernel, out_shape=jax.ShapeDtypeStruct(hidden.shape,...  95.7 us

profile of v3, /device:TPU:98, one launch (start us, length us, event | category | flops | bytes accessed | tf_op | source)
XLA Modules:
  0.0 99.0 jit_solution(2323559785384115728)
XLA Ops:
  0.7 0.3 fusion
  1.0 0.7 pad_maximum_fusion
  1.7 95.7 %attend.1 = bf16[16,3072]{1,0:T(8,128)(2,1)} custom-call(s32[1]{0:T(128)} %copy.15.len_ref, bf16[16,3072]{1,0:T(8,128)(2,1)} %x_ref.1, bf16[3072]{0:T(1024)(128)(2,1)} %gain1_ref.1, bf16[3072]{0:T(1024)(128)(2,1)} %gain2_ref.1, f32[128,128]{1,0:T(8,128)} %get-tuple-element.8.cos_ref, f32[128,128]{1,0:T(8,128)} %get-tuple-element.9.sin_ref, ...), custom_call_target="tpu_custom_call" | custom-call | tf_op jit(solution)/shard_map/attend/pallas_call | solution.py:498
  97.4 1.5 %copy.16 = bf16[16,3072]{1,0:T(8,128)(2,1)} copy(bf16[16,3072]{1,0:T(8,128)(2,1)} %attend.1) | data formatting | bytes 196608
  (2 shorter events, 0.0 us)

commit v4 on v3

--- a/solution.py
+++ b/solution.py
@@ -227,8 +227,6 @@
             c.start()
     knew[...] = rotate(dot(a, wg[:, wide : wide + HEAD_DIM]))
     vnew[...] = dot(a, wg[:, wide + HEAD_DIM : wide + 2 * HEAD_DIM]).T.astype(jnp.bfloat16)
-    for w in weights:
-        w.start()
     masks()
     for i in range(2 * RING):
         local[i].wait()
@@ -355,6 +353,8 @@
 
     q2_relay(0)
     q2_early(0)
+    for w in weights:
+        w.start()
     units = heads * 8
     advance(0, sbuf_a, top_a, None, None, None)
 
@@ -388,19 +388,16 @@
 
         @pl.when(jnp.logical_and(late, n == 2 * heads - 1))
         def _():
-            reduce_0(heads - 1, 1, True)
+            reduce_0(heads - 1, 1, False)
 
         @pl.when(jnp.logical_and(late, n >= 1))
         def _():
             reduce_1((n - 1) // 2, lax.rem(n - 1, 2))
 
-        @pl.when(jnp.logical_and(late, n >= 2))
-        def _():
-            reduce_2((n - 2) // 2, lax.rem(n - 2, 2))
-
-        @pl.when(i == units // 2 - 1)
-        def _():
-            reduce_3(0)
+        @pl.when(jnp.logical_and(late, n >= 3))
+        def _():
+            reduce_2((n - 3) // 2, lax.rem(n - 3, 2))
+
 
     cols = width // RING
     sent = []
@@ -438,10 +435,13 @@
     down_load = pltpu.make_async_copy(wd_hbm, wd, wsem.at[3])
     down_load.start()
     last = heads - 1
+    reduce_2(last - 1, 1)
+    reduce_1(last, 1)
     reduce_2(last, 0)
+    reduce_3(0)
     for g in range(1, last):
         reduce_3(g)
-    reduce_2(last, 1, True)
+    reduce_2(last, 1)
     reduce_3(last)
     keep = pl.ds(pl.multiple_of(core * (rows // 2), rows // 2), rows // 2)
     obuf[core] = ox[:, keep]

time: 100 us -> 97.1 us (0.971)
  Pallas kernels: 95.7 us -> 93 us
    pallas_call x1, Pallas kernels: 95.7 us -> 93 us  [layer(): pl.pallas_call(layer_kernel, out_shape=jax.ShapeDtypeStruct(hidden.shape,...]
where the time goes in v4:
time: 97.1 us; the launch traced here: 96.3 us
  Pallas kernels  93 us (96%)
  local copies, waits for them, and re-layouts  1.54 us (2%)
  other arithmetic  1.08 us (1%)
    pallas_call x1, Pallas kernels, layer(): pl.pallas_call(layer_kernel, out_shape=jax.ShapeDtypeStruct(hidden.shape,...  93 us

profile of v4, /device:TPU:98, one launch (start us, length us, event | category | flops | bytes accessed | tf_op | source)
XLA Modules:
  0.0 96.3 jit_solution(10836768094627081590)
XLA Ops:
  0.7 0.3 fusion
  1.0 0.7 pad_maximum_fusion
  1.7 93.0 %attend.1 = bf16[16,3072]{1,0:T(8,128)(2,1)} custom-call(s32[1]{0:T(128)} %copy.15.len_ref, bf16[16,3072]{1,0:T(8,128)(2,1)} %x_ref.1, bf16[3072]{0:T(1024)(128)(2,1)} %gain1_ref.1, bf16[3072]{0:T(1024)(128)(2,1)} %gain2_ref.1, f32[128,128]{1,0:T(8,128)} %get-tuple-element.8.cos_ref, f32[128,128]{1,0:T(8,128)} %get-tuple-element.9.sin_ref, ...), custom_call_target="tpu_custom_call" | custom-call | tf_op jit(solution)/shard_map/attend/pallas_call | solution.py:498
  94.7 1.5 %copy.16 = bf16[16,3072]{1,0:T(8,128)(2,1)} copy(bf16[16,3072]{1,0:T(8,128)(2,1)} %attend.1) | data formatting | bytes 196608
  (2 shorter events, 0.0 us)

commit v5 on v4

--- a/solution.py
+++ b/solution.py
@@ -438,10 +438,9 @@
     reduce_2(last - 1, 1)
     reduce_1(last, 1)
     reduce_2(last, 0)
-    reduce_3(0)
-    for g in range(1, last):
+    reduce_2(last, 1)
+    for g in range(last):
         reduce_3(g)
-    reduce_2(last, 1)
     reduce_3(last)
     keep = pl.ds(pl.multiple_of(core * (rows // 2), rows // 2), rows // 2)
     obuf[core] = ox[:, keep]

time: 97.1 us -> 97.1 us (level)
  no operation moved by 1% of the time
where the time goes in v5:
time: 97.1 us; the launch traced here: 96.3 us
  Pallas kernels  93 us (96%)
  local copies, waits for them, and re-layouts  1.54 us (2%)
  other arithmetic  1.08 us (1%)
    pallas_call x1, Pallas kernels, layer(): pl.pallas_call(layer_kernel, out_shape=jax.ShapeDtypeStruct(hidden.shape,...  93 us

profile of v5, /device:TPU:98, one launch (start us, length us, event | category | flops | bytes accessed | tf_op | source)
XLA Modules:
  0.0 96.3 jit_solution(3132376982231450178)
XLA Ops:
  0.7 0.3 fusion
  1.0 0.7 pad_maximum_fusion
  1.7 93.0 %attend.1 = bf16[16,3072]{1,0:T(8,128)(2,1)} custom-call(s32[1]{0:T(128)} %copy.15.len_ref, bf16[16,3072]{1,0:T(8,128)(2,1)} %x_ref.1, bf16[3072]{0:T(1024)(128)(2,1)} %gain1_ref.1, bf16[3072]{0:T(1024)(128)(2,1)} %gain2_ref.1, f32[128,128]{1,0:T(8,128)} %get-tuple-element.8.cos_ref, f32[128,128]{1,0:T(8,128)} %get-tuple-element.9.sin_ref, ...), custom_call_target="tpu_custom_call" | custom-call | tf_op jit(solution)/shard_map/attend/pallas_call | solution.py:497
  94.7 1.5 %copy.16 = bf16[16,3072]{1,0:T(8,128)(2,1)} copy(bf16[16,3072]{1,0:T(8,128)(2,1)} %attend.1) | data formatting | bytes 196608
  (2 shorter events, 0.0 us)
